TPU v7x, 256 devices: a whole 4x4x8 slice. The times are simulated.
256 devices in a mesh: ctx: 128 (over x, y_hi, z, core), head: 2 (over y_lo).
Axes of the slice: x: 4, y: 4 (y_hi: 2, y_lo: 2; y = y_hi * 2 + y_lo), z: 8, core: 2. Of those that a mesh axis runs over, the one named last changes fastest.
Arguments:
- queries: bfloat16 [16384, 2048], P('ctx', 'head'), may hold values from -160 to 160
- rotated_keys: bfloat16 [16384, 512], P('ctx', 'head'), may hold values from -6 to 6
- value_matrix: bfloat16 [16384, 512], P('ctx', 'head'), may hold values from -6 to 6
- doc_lengths: int32 [8], replicated, may hold values from 1 to 12288, 16384 in all
- scored: int32 [512], P('ctx'), may hold values from 0 to 127, as said below
- residual: bfloat16 [512, 4096], P('ctx', 'head'), may hold values from -18 to 18
- norm_gain: float32 [4096], P('head'), may hold values from 0.5 to 1.5
- out_weight: bfloat16 [2048, 4096], P('head'), may hold values from -0.5 to 0.5
- lm_weight: bfloat16 [4096, 128256], P('head', 'ctx'), may hold values from -0.40625 to 0.40625
- token_ids: int32 [512], replicated, may hold values from 0 to 128255
- old_logp: float32 [512], replicated, may hold values from -24 to -9
- advantage: float32 [512], replicated, may hold values from -3 to 3
Outputs:
- attended: bfloat16 [16384, 2048], P('ctx', 'head')
- log_probs: float32 [512], replicated
- token_loss: float32 [512], replicated
Inputs may be any that keep to these rules, and one draw needn't show every extreme that they name: `scored`: each aligned block of 4 entries holds distinct increasing offsets. `doc_lengths`: the longest document has exactly three quarters of 16384 positions.
All inputs are finite; a program needn't handle non-finite values.
Results may differ from a plain program's by a relative error of at most 0.0065.
Values may be sent and summed in bfloat16 or wider, within the bound.
No kernel may reach another device: no remote copies, remote signals or barrier semaphores. Data moves between devices by JAX's collectives and lax.ppermute only.
A program may use at most 128 MiB of HBM per device.

v0:
```python
import functools

import jax
import jax.numpy as jnp
from jax import lax
from jax.experimental import pallas as pl
from jax.experimental.pallas import tpu as pltpu
from jax.sharding import Mesh
from jax.sharding import PartitionSpec as P


HEAD_SIZE = 128
GROUP = 4
DOCS = 8
AXES = ("ctx_0", "ctx_1", "ctx_2", "ctx_3", "head")
CTX = AXES[:4]
XC = ("ctx_0", "ctx_3")
YZ = ("ctx_1", "ctx_2")
XYCH = ("ctx_0", "ctx_1", "ctx_3", "head")

LOG2E = 1.4426950408889634
SCORE_TO_LOG2 = HEAD_SIZE ** (-0.5) * LOG2E
EXTRA = 8
MASKED = -1e30
NO_TOP = -1e20


def size_of(axes):
    n = 1
    for a in axes:
        n *= lax.axis_size(a)
    return n


def spread(shard, axes):
    n = size_of(axes)
    return lax.all_to_all(
        jnp.broadcast_to(shard[None], (n, *shard.shape)), axes, 0, 0, tiled=True
    )


def swap_heads(shard):
    return lax.ppermute(shard, "head", [(0, 1), (1, 0)])


def gather_keys(meta_ref, kv_refs, k_ref, v_ref):
    x, y, z, core = [meta_ref[DOCS + n] for n in range(4)]
    groups = len(kv_refs)
    half = kv_refs[0].shape[2]
    chunk_rows = 4 * half
    v_ref[:, HEAD_SIZE:] = jnp.ones((groups * chunk_rows, HEAD_SIZE), jnp.bfloat16)
    for d in range(groups):
        place = (z - d) & (groups - 1)
        source = (x - place) & (groups // 2 - 1)
        for dy in range(2):
            base = (source * 2 + (y ^ dy)) * chunk_rows + (place // (groups // 2)) * 2 * half
            for dc in range(2):
                at = pl.multiple_of(base + (core ^ dc) * half, half)
                k_ref[pl.ds(at, half), :] = kv_refs[d][dy, dc, :, :HEAD_SIZE]
                v_ref[pl.ds(at, half), :HEAD_SIZE] = kv_refs[d][dy, dc, :, HEAD_SIZE:]


def chunk_start(meta_ref, groups, rows, i):
    return i * groups * rows + ((meta_ref[DOCS] - i // 2) & (groups // 2 - 1)) * rows


def doc_start(meta_ref, pos):
    low = jnp.zeros_like(pos)
    for d in range(DOCS):
        start = meta_ref[d]
        low = jnp.where(start <= pos, jnp.maximum(low, start), low)
    return low


def stats_of(tops, totals):
    lane = lax.broadcasted_iota(jnp.int32, tops[0].shape, 1)
    top, total = tops[0], totals[0]
    for g in range(1, GROUP):
        top = jnp.where(lane % GROUP == g, tops[g], top)
        total = jnp.where(lane % GROUP == g, totals[g], total)
    high = total.astype(jnp.bfloat16).astype(jnp.float32)
    middle = (total - high).astype(jnp.bfloat16).astype(jnp.float32)
    low = total - high - middle
    stats = jnp.where(lane < GROUP, top, high)
    stats = jnp.where(lane >= 2 * GROUP, middle, stats)
    stats = jnp.where(lane >= 3 * GROUP, low, stats)
    return jnp.where(lane >= 4 * GROUP, 0.0, stats).astype(jnp.bfloat16)


def query_kernel(scored_ref, q_ref, out_ref):
    rows = q_ref.shape[0]
    width = out_ref.shape[2]
    count = scored_ref.shape[0]
    row = lax.broadcasted_iota(jnp.int32, (EXTRA, rows), 0)
    col = lax.broadcasted_iota(jnp.int32, (EXTRA, rows), 1)
    wide = lax.broadcasted_iota(jnp.int32, (EXTRA, width), 0)
    pick = jnp.zeros((EXTRA, rows), jnp.float32)
    offsets = jnp.zeros((EXTRA, width), jnp.int32)
    for i in range(count):
        pick = jnp.where((row == i) & (col == scored_ref[i]), 1.0, pick)
        offsets = jnp.where(wide == EXTRA // 2 + i, scored_ref[i], offsets)
    pick = pick.astype(jnp.bfloat16)
    offsets = offsets.astype(jnp.float32)
    for c in range(2):
        heads = q_ref[:, c * width : (c + 1) * width]
        extra = jnp.dot(pick, heads, preferred_element_type=jnp.float32) + offsets
        for n in range(out_ref.shape[0] // 2):
            out_ref[2 * n + c, :rows] = heads
            out_ref[2 * n + c, rows:] = extra.astype(jnp.bfloat16)


def queries_to_send(scored, queries, copies):
    rows, features = queries.shape
    return pl.pallas_call(
        query_kernel,
        in_specs=[
            pl.BlockSpec(memory_space=pltpu.SMEM),
            pl.BlockSpec(memory_space=pltpu.VMEM),
        ],
        out_specs=pl.BlockSpec(memory_space=pltpu.VMEM),
        out_shape=jax.ShapeDtypeStruct((2 * copies, rows + EXTRA, features // 2), jnp.bfloat16),
        name="queries_to_send",
    )(scored, queries)


def chosen_kernel(meta_ref, q_ref, *refs):
    groups = len(refs) - 6
    kv_refs = refs[:groups]
    out_ref, k_ref, v_ref, m_ref, acc_ref, s_ref = refs[groups:]
    half = kv_refs[0].shape[2]
    rows = 2 * half
    span = groups * rows
    chunks, lines, chunk_rows = s_ref.shape
    peers = q_ref.shape[0]
    each = lines // GROUP
    y, z = meta_ref[DOCS + 1], meta_ref[DOCS + 2]
    gather_keys(meta_ref, kv_refs, k_ref, v_ref)
    wide = q_ref[...].astype(jnp.float32)
    offset = pltpu.roll(wide[:, :, :HEAD_SIZE], EXTRA // 2, 1).astype(jnp.int32)
    peer = lax.broadcasted_iota(jnp.int32, offset.shape, 0)
    pos = (2 * (peer // 2) + y) * span + z * rows + (peer % 2) * half + offset
    pos = pos.reshape(each, HEAD_SIZE)
    low = doc_start(meta_ref, pos)
    q = jnp.concatenate(
        [
            wide[:, :, g * HEAD_SIZE : (g + 1) * HEAD_SIZE].reshape(each, HEAD_SIZE)
            for g in range(GROUP)
        ]
    ).astype(jnp.bfloat16)
    pos = jnp.concatenate([pos] * GROUP)
    low = jnp.concatenate([low] * GROUP)
    m_ref[...] = jnp.full(m_ref.shape, NO_TOP, jnp.float32)
    acc_ref[...] = jnp.zeros(acc_ref.shape, jnp.float32)

    def score_step(i, carry):
        at = pl.multiple_of(i * chunk_rows, chunk_rows)
        s = lax.dot_general(
            q,
            k_ref[pl.ds(at, chunk_rows), :],
            (((1,), (1,)), ((), ())),
            preferred_element_type=jnp.float32,
        )
        base = chunk_start(meta_ref, groups, rows, i)
        top = m_ref[...]
        for h in range(chunk_rows // HEAD_SIZE):
            start = h * HEAD_SIZE
            if start >= rows:
                start += span // 2 - rows
            key = lax.broadcasted_iota(jnp.int32, pos.shape, 1) + (base + start)
            part = jnp.where(
                (key >= low) & (key <= pos), s[:, h * HEAD_SIZE : (h + 1) * HEAD_SIZE], MASKED
            )
            s_ref[i, :, h * HEAD_SIZE : (h + 1) * HEAD_SIZE] = part
            top = jnp.maximum(top, part)
        m_ref[...] = top
        return carry

    lax.fori_loop(0, chunks, score_step, 0)
    top = jnp.max(m_ref[...], axis=1, keepdims=True) * SCORE_TO_LOG2
    top = jnp.maximum(top, NO_TOP).astype(jnp.bfloat16).astype(jnp.float32)
    top = jnp.broadcast_to(top, m_ref.shape)
    m_ref[...] = top

    def weigh_step(i, carry):
        at = pl.multiple_of(i * chunk_rows, chunk_rows)
        tops = jnp.concatenate([m_ref[...]] * (chunk_rows // HEAD_SIZE), axis=1)
        p = jnp.exp2(s_ref[i] * SCORE_TO_LOG2 - tops).astype(jnp.bfloat16)
        acc_ref[...] += jnp.dot(
            p, v_ref[pl.ds(at, chunk_rows), :], preferred_element_type=jnp.float32
        )
        return carry

    lax.fori_loop(0, chunks, weigh_step, 0)
    tops, totals = [], []
    for g in range(GROUP):
        at = slice(g * each, (g + 1) * each)
        out_ref[:, :, g * HEAD_SIZE : (g + 1) * HEAD_SIZE] = (
            acc_ref[at, :HEAD_SIZE].reshape(peers, EXTRA, HEAD_SIZE).astype(jnp.bfloat16)
        )
        tops.append(m_ref[at])
        totals.append(acc_ref[at, HEAD_SIZE:])
    out_ref[:, :, GROUP * HEAD_SIZE :] = stats_of(tops, totals).reshape(peers, EXTRA, HEAD_SIZE)


def chosen_attention(meta, q_all, kv_all):
    peers, tall, width = q_all.shape
    half = tall - EXTRA
    chunk_rows = 4 * half
    keys = chunk_rows * len(kv_all)
    lines = GROUP * peers * EXTRA
    wide = width + HEAD_SIZE
    return pl.pallas_call(
        chosen_kernel,
        grid_spec=pltpu.PrefetchScalarGridSpec(
            num_scalar_prefetch=1,
            grid=(1,),
            in_specs=[pl.BlockSpec((peers, EXTRA, width), lambda j, meta: (0, half // EXTRA, 0))]
            + [pl.BlockSpec((2, 2, half, 2 * HEAD_SIZE), lambda j, meta: (0, 0, 0, 0))]
            * len(kv_all),
            out_specs=pl.BlockSpec((peers, EXTRA, wide), lambda j, meta: (0, 0, 0)),
            scratch_shapes=[
                pltpu.VMEM((keys, HEAD_SIZE), jnp.bfloat16),
                pltpu.VMEM((keys, 2 * HEAD_SIZE), jnp.bfloat16),
                pltpu.VMEM((lines, HEAD_SIZE), jnp.float32),
                pltpu.VMEM((lines, 2 * HEAD_SIZE), jnp.float32),
                pltpu.VMEM((keys // chunk_rows, lines, chunk_rows), jnp.float32),
            ],
        ),
        out_shape=jax.ShapeDtypeStruct((peers, EXTRA, wide), jnp.bfloat16),
        name="chosen_attention",
    )(meta, q_all, *kv_all)


def attention_kernel(first_block, meta_ref, q_ref, *refs):
    groups = len(refs) - 7
    kv_refs = refs[:groups]
    out_ref, k_ref, v_ref, m_ref, acc_ref, s_ref = refs[groups + 1 :]
    j = pl.program_id(0) + first_block
    half = out_ref.shape[1]
    rows = 2 * half
    chunk_rows = s_ref.shape[3]
    chunks = s_ref.shape[1]
    y, z = meta_ref[DOCS + 1], meta_ref[DOCS + 2]
    span = groups * rows

    @pl.when(j == first_block)
    def _():
        gather_keys(meta_ref, kv_refs, k_ref, v_ref)

    first_q = (2 * j + y) * span + z * rows
    last_q = first_q + rows - 1
    far = span // 2
    reach = far + rows - 1

    chunk_base = functools.partial(chunk_start, meta_ref, groups, rows)
    low_first = doc_start(meta_ref, first_q)
    low_last = doc_start(meta_ref, last_q)
    m_ref[...] = jnp.full(m_ref.shape, NO_TOP, jnp.float32)
    acc_ref[...] = jnp.zeros(acc_ref.shape, jnp.float32)
    chunk_lo, chunk_hi = jnp.int32(0), jnp.int32(0)
    for i in range(chunks):
        base = chunk_base(i)
        chunk_lo += (base + reach < low_first).astype(jnp.int32)
        chunk_hi += (base <= last_q).astype(jnp.int32)

    def score(i, masked):
        at = pl.multiple_of(i * chunk_rows, chunk_rows)
        k = k_ref[pl.ds(at, chunk_rows), :]
        if masked:
            pos = first_q + lax.broadcasted_iota(jnp.int32, (rows, 1), 0)
            low = doc_start(meta_ref, pos)
            base = chunk_base(i)
            key = lax.broadcasted_iota(jnp.int32, (rows, chunk_rows), 1)
            key = key + jnp.where(key >= rows, far - rows, 0)
            allowed = (key >= low - base) & (key <= pos - base)
        for g in range(GROUP):
            q = q_ref[:, :, g * HEAD_SIZE : (g + 1) * HEAD_SIZE].reshape(rows, HEAD_SIZE)
            s = lax.dot_general(
                q, k, (((1,), (1,)), ((), ())), preferred_element_type=jnp.float32
            )
            if masked:
                s = jnp.where(allowed, s, MASKED)
            s_ref[g, i] = s
            top = m_ref[g]
            for h in range(chunk_rows // HEAD_SIZE):
                top = jnp.maximum(top, s[:, h * HEAD_SIZE : (h + 1) * HEAD_SIZE])
            m_ref[g] = top

    def score_step(i, carry):
        base = chunk_base(i)
        free = (base >= low_last) & (base + reach <= first_q)

        @pl.when(free)
        def _():
            score(i, False)

        @pl.when(jnp.logical_not(free))
        def _():
            score(i, True)

        return carry

    lax.fori_loop(chunk_lo, chunk_hi, score_step, 0)
    for g in range(GROUP):
        top = jnp.max(m_ref[g], axis=1, keepdims=True) * SCORE_TO_LOG2
        top = jnp.maximum(top, NO_TOP).astype(jnp.bfloat16).astype(jnp.float32)
        m_ref[g] = jnp.broadcast_to(top, (rows, HEAD_SIZE))

    def weigh_step(i, carry):
        at = pl.multiple_of(i * chunk_rows, chunk_rows)
        v = v_ref[pl.ds(at, chunk_rows), :]
        for g in range(GROUP):
            top = m_ref[g]
            top = jnp.concatenate([top] * (chunk_rows // HEAD_SIZE), axis=1)
            p = jnp.exp2(s_ref[g, i] * SCORE_TO_LOG2 - top).astype(jnp.bfloat16)
            acc_ref[g] += jnp.dot(p, v, preferred_element_type=jnp.float32)
        return carry

    lax.fori_loop(chunk_lo, chunk_hi, weigh_step, 0)

    for g in range(GROUP):
        out_ref[:, :, g * HEAD_SIZE : (g + 1) * HEAD_SIZE] = (
            acc_ref[g, :, :HEAD_SIZE].astype(jnp.bfloat16).reshape(2, half, HEAD_SIZE)
        )
    stats = stats_of(
        [m_ref[g] for g in range(GROUP)], [acc_ref[g, :, HEAD_SIZE:] for g in range(GROUP)]
    )
    out_ref[:, :, GROUP * HEAD_SIZE :] = stats.reshape(2, half, HEAD_SIZE)


def partial_attention(meta, q_all, kv_all, first, number, before):
    peers, tall, width = q_all.shape
    half = tall - EXTRA
    rows = 2 * half
    chunk_rows = 2 * rows
    keys = chunk_rows * len(kv_all)
    wide = width + HEAD_SIZE
    at = lambda j, meta: (j + first, 0, 0)
    return pl.pallas_call(
        functools.partial(attention_kernel, first),
        grid_spec=pltpu.PrefetchScalarGridSpec(
            num_scalar_prefetch=1,
            grid=(number,),
            in_specs=[pl.BlockSpec((2, half, width), at)]
            + [pl.BlockSpec((2, 2, half, 2 * HEAD_SIZE), lambda j, meta: (0, 0, 0, 0))]
            * len(kv_all)
            + [pl.BlockSpec(memory_space=pl.ANY)],
            out_specs=pl.BlockSpec((2, half, wide), at),
            scratch_shapes=[
                pltpu.VMEM((keys, HEAD_SIZE), jnp.bfloat16),
                pltpu.VMEM((keys, 2 * HEAD_SIZE), jnp.bfloat16),
                pltpu.VMEM((GROUP, rows, HEAD_SIZE), jnp.float32),
                pltpu.VMEM((GROUP, rows, 2 * HEAD_SIZE), jnp.float32),
                pltpu.VMEM((GROUP, keys // chunk_rows, rows, chunk_rows), jnp.float32),
            ],
        ),
        out_shape=jax.ShapeDtypeStruct((peers, half, wide), jnp.bfloat16),
        input_output_aliases={2 + len(kv_all): 0} if first else {},
        compiler_params=pltpu.CompilerParams(dimension_semantics=("arbitrary",)),
        cost_estimate=pl.CostEstimate(
            flops=number * 5 * 10**9, bytes_accessed=4 * 10**6, transcendentals=0
        ),
        name="partial_attention",
    )(meta, q_all, *kv_all, before)


def merge_kernel(parts_ref, merged_ref):
    windows = parts_ref.shape[0] // 2
    rows = parts_ref.shape[1]
    for c in range(2):
        tops, sums = [], []
        for w in range(windows):
            st = parts_ref[2 * w + c, :, GROUP * HEAD_SIZE :].astype(jnp.float32)
            tops.append(st)
            sums.append(
                pltpu.roll(st, HEAD_SIZE - GROUP, 1)
                + pltpu.roll(st, HEAD_SIZE - 2 * GROUP, 1)
                + pltpu.roll(st, HEAD_SIZE - 3 * GROUP, 1)
            )
        top = functools.reduce(jnp.maximum, tops)
        shares = [jnp.exp2(t - top) for t in tops]
        total = functools.reduce(jnp.add, [n * share for n, share in zip(sums, shares)])
        lane = lax.broadcasted_iota(jnp.int32, total.shape, 1)
        total = jnp.where((lane < GROUP) & (total > 0.0), total, 1.0)
        shares = [share / total for share in shares]
        for g in range(GROUP):
            result = jnp.zeros((rows, HEAD_SIZE), jnp.float32)
            for w in range(windows):
                part = parts_ref[2 * w + c, :, g * HEAD_SIZE : (g + 1) * HEAD_SIZE]
                result = result + shares[w][:, g : g + 1] * part.astype(jnp.float32)
            at = (c * GROUP + g) * HEAD_SIZE
            merged_ref[:, at : at + HEAD_SIZE] = result.astype(jnp.bfloat16)


def merged_attention(parts):
    rows = parts.shape[1]
    return pl.pallas_call(
        merge_kernel,
        in_specs=[pl.BlockSpec(memory_space=pltpu.VMEM)],
        out_specs=pl.BlockSpec(memory_space=pltpu.VMEM),
        out_shape=jax.ShapeDtypeStruct((rows, 2 * GROUP * HEAD_SIZE), jnp.bfloat16),
    )(parts)


def merged_stats(stats, axis):
    tops, sums, targets = stats
    top = jnp.max(tops, axis=axis)
    total = jnp.sum(sums * jnp.exp(tops - jnp.expand_dims(top, axis)), axis=axis)
    return (top, total, jnp.sum(targets, axis=axis))


def per_device(
    queries,
    rotated_keys,
    value_matrix,
    doc_lengths,
    scored,
    residual,
    norm_gain,
    out_weight,
    lm_weight,
    token_ids,
    old_logp,
    advantage,
):
    count = scored.shape[0]
    nx, ny, nz, cores = [lax.axis_size(a) for a in CTX]
    x, y, z, core = [lax.axis_index(a) for a in CTX]
    doc_starts = jnp.cumsum(doc_lengths) - doc_lengths
    meta = jnp.concatenate(
        [doc_starts.astype(jnp.int32), jnp.stack([x, y, z, core]).astype(jnp.int32)]
    )

    def of_head(c):
        at = c * HEAD_SIZE
        return jnp.concatenate(
            [
                lax.dynamic_slice_in_dim(rotated_keys, at, HEAD_SIZE, 1),
                lax.dynamic_slice_in_dim(value_matrix, at, HEAD_SIZE, 1),
            ],
            axis=1,
        )

    def handed(dy, dc):
        return [
            (
                ((i * ny + k) * nz + l) * cores + c,
                ((((i + l) % nx) * ny + (k ^ dy)) * nz + l) * cores + (c ^ dc),
            )
            for i in range(nx)
            for k in range(ny)
            for l in range(nz)
            for c in range(cores)
        ]

    mine, others = of_head(core), of_head(1 - core)
    own = jnp.stack(
        [
            jnp.stack([lax.ppermute(mine, CTX, handed(dy, 0)), lax.ppermute(others, CTX, handed(dy, 1))])
            for dy in range(ny)
        ]
    )

    def shifted(a, d):
        return lax.ppermute(a, "ctx_2", [(k, (k + d) % nz) for k in range(nz)])

    kv_all = [own] + [None] * (nz - 1)
    for d in range(1, nz // 2):
        kv_all[d] = shifted(kv_all[d - 1], 1)
        kv_all[nz - d] = shifted(kv_all[(nz - d + 1) % nz], -1)
    far = nz // 2
    kv_all[far] = jnp.stack([shifted(kv_all[far - 1][0], 1), shifted(kv_all[far + 1][1], -1)])

    q_send = queries_to_send(scored, queries, nx)
    q_all = lax.all_to_all(q_send, XC, 0, 0, tiled=True)
    few = chosen_attention(meta, q_all, kv_all)
    few = lax.all_to_all(few, XC, 0, 0, tiled=True)
    chosen = merged_attention(few)
    parts = partial_attention(meta, q_all, kv_all, 0, nx // 2, q_all)
    parts = partial_attention(meta, q_all, kv_all, nx // 2, nx - nx // 2, parts)
    arrived = lax.all_to_all(parts, XC, 0, 0, tiled=True)
    attended = merged_attention(arrived)

    half = residual.shape[1]
    head = lax.axis_index("head")
    partial_value = jnp.dot(chosen, out_weight, preferred_element_type=jnp.float32)[:count]
    own = lax.dynamic_slice_in_dim(partial_value, head * half, half, 1)
    own = own + residual.astype(jnp.float32)
    partial_value = lax.dynamic_update_slice_in_dim(partial_value, own, head * half, 1)
    other = swap_heads(partial_value.astype(jnp.bfloat16)).astype(jnp.float32)
    hidden_all = partial_value + other
    squares = jnp.sum(hidden_all * hidden_all, axis=1, keepdims=True)
    hidden = own + lax.dynamic_slice_in_dim(other, head * half, half, 1)
    normed = (
        hidden * lax.rsqrt(squares / hidden_all.shape[1] + 1e-05) * norm_gain[None, :]
    ).astype(jnp.bfloat16)

    along_yz = spread(normed, YZ)
    own_rows = spread(along_yz, ("ctx_0",)).reshape(-1, half)
    other_rows = lax.ppermute(own_rows, "ctx_3", [(0, 1), (1, 0)])
    rows = own_rows.shape[0] // 2
    chips = nx * ny * nz
    vocab_rows = lm_weight.shape[1]
    my_index = ((x * ny + y) * nz + z) * cores + core
    ids = token_ids.reshape(chips, cores, count).swapaxes(0, 1).reshape(cores, 2, rows)
    ids = lax.dynamic_index_in_dim(ids, head, 1, keepdims=False) - my_index * vocab_rows

    def local_stats(normed_rows, local_ids):
        partial_logits = jnp.dot(normed_rows, lm_weight, preferred_element_type=jnp.float32)
        theirs = lax.dynamic_slice_in_dim(partial_logits, (1 - head) * rows, rows, 0)
        ours = lax.dynamic_slice_in_dim(partial_logits, head * rows, rows, 0)
        logits = ours + swap_heads(theirs.astype(jnp.bfloat16)).astype(jnp.float32)
        matches = local_ids[:, None] == jnp.arange(vocab_rows, dtype=jnp.int32)[None, :]
        target_part = jnp.sum(jnp.where(matches, logits, 0.0), axis=1)
        local_top = jnp.max(logits, axis=1)
        sum_part = jnp.sum(jnp.exp(logits - local_top[:, None]), axis=1)
        return jnp.stack([local_top, sum_part, target_part])

    ids_first = lax.dynamic_index_in_dim(ids, core, 0, keepdims=False)
    ids_second = lax.dynamic_index_in_dim(ids, 1 - core, 0, keepdims=False)
    first = local_stats(own_rows, ids_first)
    second = local_stats(other_rows, ids_second)
    stats = jnp.where(core == 0, jnp.stack([first, second]), jnp.stack([second, first]))
    by_z = spread(stats, ("ctx_2",))
    merged = merged_stats((by_z[:, :, 0], by_z[:, :, 1], by_z[:, :, 2]), 0)
    by_rest = spread(jnp.stack(merged), XYCH)
    by_rest = by_rest.reshape(-1, 2, 3, cores, rows)
    top, total, target = merged_stats((by_rest[:, :, 0], by_rest[:, :, 1], by_rest[:, :, 2]), 0)
    log_probs = (target - top - jnp.log(total)).reshape(2, cores, rows // count, count)
    log_probs = log_probs.swapaxes(1, 2).reshape(chips * cores * count)
    ratio = jnp.exp(jnp.clip(log_probs - old_logp, -4.0, 4.0))
    token_loss = -jnp.minimum(ratio * advantage, jnp.clip(ratio, 0.8, 1.2) * advantage)
    return (attended, log_probs, token_loss)


def solution(mesh):
    finer = Mesh(mesh.devices.reshape(4, 2, 8, 2, mesh.shape["head"]), AXES)
    ctx = AXES[:4]
    placed = (
        P(ctx, "head"),
        P(ctx, "head"),
        P(ctx, "head"),
        P(),
        P(ctx),
        P(ctx, "head"),
        P("head"),
        P("head", None),
        P("head", ctx),
        P(),
        P(),
        P(),
    )

    return jax.shard_map(
        per_device,
        mesh=finer,
        in_specs=placed,
        out_specs=(P(ctx, "head"), P(), P()),
        check_vma=False,
    )
```

profile of v0, /device:TPU:1, one launch (start us, length us, event | category | flops | bytes accessed | tf_op | source)
XLA Modules:
  0.0 203.8 jit_solution(942964540053136634)
XLA Ops:
  0.6 0.8 constant_dynamic-slice_fusion.5
  1.5 4.4 %collective-permute-start.3 = (bf16[128,256]{1,0:T(8,128)(2,1)S(1)}, bf16[128,256]{1,0:T(8,128)(2,1)S(1)}, u32[]{:S(2)}, u32[]{:S(2)}) collective-permute-start(bf16[128,256]{1,0:T(8,128)(2,1)S(1)} %pad_maximum_fusion.3), channel_id=1, source_target_pairs={{0,34},{2,32},{4,102},{6,100},{8,170},{10,168},{12,238},{14,236},{... | collective-permute-start | bytes 196616 | tf_op jit(solution)/shard_map/ppermute | solution.py:459
  5.9 1.9 collective-permute-start.2
  7.7 0.7 collective-permute-start
  8.4 2.9 %collective-permute-done.2 = bf16[128,256]{1,0:T(8,128)(2,1)S(1)} collective-permute-done((bf16[128,256]{1,0:T(8,128)(2,1)S(1)}, bf16[128,256]{1,0:T(8,128)(2,1)S(1)}, u32[]{:S(2)}, u32[]{:S(2)}) %collective-permute-start.2) | collective-permute-done | bytes 65568 | tf_op jit(solution)/shard_map/ppermute | solution.py:459
  11.4 8.7 %collective-permute-start.8 = (bf16[2,2,128,256]{3,2,1,0:T(8,128)(2,1)S(1)}, bf16[2,2,128,256]{3,2,1,0:T(8,128)(2,1)S(1)}, u32[]{:S(2)}, u32[]{:S(2)}) collective-permute-start(bf16[2,2,128,256]{3,2,1,0:T(8,128)(2,1)S(1)} %pad_maximum_fusion.refs_0_), channel_id=1, source_target_pairs={{0,28},{4,0},{8,4},{12,8},{16,12},{20,16},{24,20},{28,24},{1,29},{... | collective-permute-start | bytes 786440 | tf_op jit(solution)/shard_map/ppermute | solution.py:465
  20.1 4.7 %collective-permute-done.8.refs_7_ = bf16[2,2,128,256]{3,2,1,0:T(8,128)(2,1)S(1)} collective-permute-done((bf16[2,2,128,256]{3,2,1,0:T(8,128)(2,1)S(1)}, bf16[2,2,128,256]{3,2,1,0:T(8,128)(2,1)S(1)}, u32[]{:S(2)}, u32[]{:S(2)}) %collective-permute-start.8) | collective-permute-done | bytes 262176 | tf_op jit(solution)/shard_map/ppermute | solution.py:465
  24.8 3.4 %collective-permute-start.9 = (bf16[2,2,128,256]{3,2,1,0:T(8,128)(2,1)S(1)}, bf16[2,2,128,256]{3,2,1,0:T(8,128)(2,1)S(1)}, u32[]{:S(2)}, u32[]{:S(2)}) collective-permute-start(bf16[2,2,128,256]{3,2,1,0:T(8,128)(2,1)S(1)} %collective-permute-done.8.refs_7_), channel_id=1, source_target_pairs={{0,28},{4,0},{8,4},{12,8},{16,12},{20,16},{24,20},{28,24},{1,29},{... | collective-permute-start | bytes 786440 | tf_op jit(solution)/shard_map/ppermute | solution.py:465
  28.2 0.7 collective-permute-done.4.refs_1_
  29.0 2.6 %collective-permute-done.9.refs_6_ = bf16[2,2,128,256]{3,2,1,0:T(8,128)(2,1)S(1)} collective-permute-done((bf16[2,2,128,256]{3,2,1,0:T(8,128)(2,1)S(1)}, bf16[2,2,128,256]{3,2,1,0:T(8,128)(2,1)S(1)}, u32[]{:S(2)}, u32[]{:S(2)}) %collective-permute-start.9) | collective-permute-done | bytes 262176 | tf_op jit(solution)/shard_map/ppermute | solution.py:465
  31.6 3.1 %collective-permute-start.10 = (bf16[2,2,128,256]{3,2,1,0:T(8,128)(2,1)S(1)}, bf16[2,2,128,256]{3,2,1,0:T(8,128)(2,1)S(1)}, u32[]{:S(2)}, u32[]{:S(2)}) collective-permute-start(bf16[2,2,128,256]{3,2,1,0:T(8,128)(2,1)S(1)} %collective-permute-done.9.refs_6_), channel_id=1, source_target_pairs={{0,28},{4,0},{8,4},{12,8},{16,12},{20,16},{24,20},{28,24},{1,29},{... | collective-permute-start | bytes 786440 | tf_op jit(solution)/shard_map/ppermute | solution.py:465
  34.7 2.1 %queries_to_send.1 = bf16[8,136,512]{2,1,0:T(8,128)(2,1)} custom-call(s32[4]{0:T(128)} %scored_ref.1, bf16[128,1024]{1,0:T(8,128)(2,1)} %q_ref.1), custom_call_target="tpu_custom_call" | custom-call | tf_op jit(solution)/shard_map/queries_to_send/pallas_call | solution.py:114
  36.8 9.0 %all-to-all-start = ((bf16[8,136,512]{2,1,0:T(8,128)(2,1)}), bf16[8,136,512]{2,1,0:T(8,128)(2,1)S(1)}, u32[]{:S(2)}, u32[]{:S(2)}) async-start(bf16[8,136,512]{2,1,0:T(8,128)(2,1)} %queries_to_send.1), calls=%async_computation | async-start | bytes 2228224 | tf_op jit(solution)/shard_map/all_to_all | solution.py:475
  46.2 2.7 %collective-permute-start.11 = (bf16[2,128,256]{2,1,0:T(8,128)(2,1)S(1)}, bf16[2,128,256]{2,1,0:T(8,128)(2,1)S(1)}, u32[]{:S(2)}, u32[]{:S(2)}) collective-permute-start(bf16[2,128,256]{2,1,0:T(8,128)(2,1)S(1)} %slice_bitcast_fusion), channel_id=1, source_target_pairs={{0,28},{4,0},{8,4},{12,8},{16,12},{20,16},{24,20},{28,24},{1,29},{... | collective-permute-start | bytes 393224 | tf_op jit(solution)/shard_map/ppermute | solution.py:465
  48.9 6.1 %collective-permute-done.6.refs_3_ = bf16[2,2,128,256]{3,2,1,0:T(8,128)(2,1)S(1)} collective-permute-done((bf16[2,2,128,256]{3,2,1,0:T(8,128)(2,1)S(1)}, bf16[2,2,128,256]{3,2,1,0:T(8,128)(2,1)S(1)}, u32[]{:S(2)}, u32[]{:S(2)}) %collective-permute-start.6) | collective-permute-done | bytes 262176 | tf_op jit(solution)/shard_map/ppermute | solution.py:465
  55.1 0.6 concatenate.17.meta_ref
  55.8 4.7 %collective-permute-done.7 = bf16[2,128,256]{2,1,0:T(8,128)(2,1)S(1)} collective-permute-done((bf16[2,128,256]{2,1,0:T(8,128)(2,1)S(1)}, bf16[2,128,256]{2,1,0:T(8,128)(2,1)S(1)}, u32[]{:S(2)}, u32[]{:S(2)}) %collective-permute-start.7) | collective-permute-done | bytes 131104 | tf_op jit(solution)/shard_map/ppermute | solution.py:465
  60.5 0.7 pad_maximum_fusion.1.refs_4_
  61.2 0.3 all-to-all-done.q_ref.refs_8_
  61.6 1.0 copy-done.1
  62.6 7.3 %chosen_attention.1 = bf16[8,8,640]{2,1,0:T(8,128)(2,1)} custom-call(s32[12]{0:T(128)} %concatenate.17.meta_ref, bf16[8,136,512]{2,1,0:T(8,128)(2,1)} %copy-done.1, bf16[2,2,128,256]{3,2,1,0:T(8,128)(2,1)} %copy-done.2, bf16[2,2,128,256]{3,2,1,0:T(8,128)(2,1)} %copy-done.7, bf16[2,2,128,256]{3,2,1,0:T(8,128)(2,1)} %copy-done.9, ...), custom_call_target="tpu_custom_call" | custom-call | tf_op jit(solution)/shard_map/chosen_attention/pallas_call | solution.py:212
  69.9 5.8 %all-to-all-start.2 = ((bf16[8,8,640]{2,1,0:T(8,128)(2,1)}), bf16[8,8,640]{2,1,0:T(8,128)(2,1)S(1)}, u32[]{:S(2)}, u32[]{:S(2)}) async-start(bf16[8,8,640]{2,1,0:T(8,128)(2,1)} %chosen_attention.1), calls=%async_computation.2 | async-start | bytes 163840 | tf_op jit(solution)/shard_map/all_to_all | solution.py:477
  75.7 4.9 %all-to-all-done.2.parts_ref = bf16[8,8,640]{2,1,0:T(8,128)(2,1)S(1)} async-done(((bf16[8,8,640]{2,1,0:T(8,128)(2,1)}), bf16[8,8,640]{2,1,0:T(8,128)(2,1)S(1)}, u32[]{:S(2)}, u32[]{:S(2)}) %all-to-all-start.2) | async-done | bytes 81952 | tf_op jit(solution)/shard_map/all_to_all | solution.py:477
  80.6 0.6 copy-done.5
  81.2 1.7 shard_map.140
  82.9 4.6 %fusion.8 = f32[4,4096]{1,0:T(4,128)S(1)} fusion(bf16[1024,4096]{1,0:T(8,128)(2,1)} %param.19, bf16[8,1024]{1,0:T(8,128)(2,1)} %shard_map.140), kind=kOutput, calls=%fused_computation.35 | convolution fusion | flops 33554432 | bytes 8462336 | tf_op jit(solution)/shard_map/dot_general | solution.py:486
  87.7 2.8 %collective-permute-done.12 = bf16[4,4096]{1,0:T(4,128)(2,1)S(1)} collective-permute-done((bf16[4,4096]{1,0:T(4,128)(2,1)S(1)}, bf16[4,4096]{1,0:T(4,128)(2,1)S(1)}, u32[]{:S(2)}, u32[]{:S(2)}) %collective-permute-start.12) | collective-permute-done | bytes 32800 | tf_op jit(solution)/shard_map/ppermute | solution.py:43
  90.8 12.4 %all_to_all.35 = bf16[16,4,2048]{2,1,0:T(4,128)(2,1)S(1)} all-to-all(bf16[16,4,2048]{2,1,0:T(4,128)(2,1)S(1)} %broadcast_in_dim.12), channel_id=1, replica_groups=mesh['ctx_0'=4,'ctx_1'=2,'ctx_2'=8,'ctx_3'=2,'head'=2] {'ctx_1','ctx_2'}, dimensions={0} | all-to-all | bytes 524288 | tf_op jit(solution)/shard_map/all_to_all | solution.py:37
  103.2 1.5 broadcast_in_dim.14
  104.7 3.5 %all-to-all-start.4 = ((bf16[4,16,4,2048]{3,2,1,0:T(4,128)(2,1)}), bf16[4,16,4,2048]{3,2,1,0:T(4,128)(2,1)S(1)}, u32[]{:S(2)}, u32[]{:S(2)}) async-start(bf16[4,16,4,2048]{3,2,1,0:T(4,128)(2,1)} %broadcast_in_dim.14), calls=%async_computation.4 | async-start | bytes 2097152 | tf_op jit(solution)/shard_map/all_to_all | solution.py:37
  108.6 11.1 %all-to-all-done.4 = bf16[4,16,4,2048]{3,2,1,0:T(4,128)(2,1)S(1)} async-done(((bf16[4,16,4,2048]{3,2,1,0:T(4,128)(2,1)}), bf16[4,16,4,2048]{3,2,1,0:T(4,128)(2,1)S(1)}, u32[]{:S(2)}, u32[]{:S(2)}) %all-to-all-start.4) | async-done | bytes 1048608 | tf_op jit(solution)/shard_map/all_to_all | solution.py:37
  119.9 4.7 %collective-permute-start.14 = (bf16[256,2048]{1,0:T(8,128)(2,1)S(1)}, bf16[256,2048]{1,0:T(8,128)(2,1)}, u32[]{:S(2)}, u32[]{:S(2)}) collective-permute-start(bf16[256,2048]{1,0:T(8,128)(2,1)S(1)} %reshape.115), channel_id=1, source_target_pairs={{0,2},{2,0},{1,3},{3,1},{4,6},{6,4},{5,7},{7,5},{8,10},{10,8},{9,1... | collective-permute-start | bytes 3145736 | tf_op jit(solution)/shard_map/ppermute | solution.py:500
  124.6 3.5 %fusion.15 = f32[256,1002]{0,1:T(8,128)S(1)} fusion(bf16[256,2048]{1,0:T(8,128)(2,1)S(1)} %reshape.115, bf16[2048,1002]{0,1:T(8,128)(2,1)} %param.20), kind=kOutput, calls=%fused_computation.60 | convolution fusion | flops 1050673152 | bytes 6178816 | tf_op jit(solution)/shard_map/dot_general | solution.py:509
  128.2 0.5 collective-permute-start.13
  128.6 7.4 %partial_attention.2.refs_8_ = bf16[8,128,640]{2,1,0:T(8,128)(2,1)} custom-call(s32[12]{0:T(128)} %concatenate.17.meta_ref, bf16[8,136,512]{2,1,0:T(8,128)(2,1)} %copy-done.1, bf16[2,2,128,256]{3,2,1,0:T(8,128)(2,1)} %copy-done.2, bf16[2,2,128,256]{3,2,1,0:T(8,128)(2,1)} %copy-done.7, bf16[2,2,128,256]{3,2,1,0:T(8,128)(2,1)} %copy-done.9, ...), custom_call_target="tpu_custom_call" | custom-call | flops 10000000000 | bytes 4000000 | tf_op jit(solution)/shard_map/partial_attention/pallas_call | solution.py:339
  136.2 3.8 %fusion.16 = f32[256,1002]{0,1:T(8,128)S(1)} fusion(bf16[256,2048]{1,0:T(8,128)(2,1)} %collective-permute-done.14, bf16[2048,1002]{0,1:T(8,128)(2,1)} %param.20), kind=kOutput, calls=%fused_computation.61 | convolution fusion | flops 1050673152 | bytes 6178816 | tf_op jit(solution)/shard_map/dot_general | solution.py:509
  140.0 1.2 collective-permute-start.15
  141.4 5.7 %collective-permute-done.15 = bf16[128,1002]{0,1:T(8,128)(2,1)S(1)} collective-permute-done((bf16[128,1002]{0,1:T(8,128)(2,1)S(1)}, bf16[128,1002]{0,1:T(8,128)(2,1)S(1)}, u32[]{:S(2)}, u32[]{:S(2)}) %collective-permute-start.15) | collective-permute-done | bytes 256544 | tf_op jit(solution)/shard_map/ppermute | solution.py:43
  147.5 0.6 broadcast_in_dim.16
  148.1 5.4 %all-to-all-start.5 = ((f32[8,2,3,128]{3,1,2,0:T(2,128)}), f32[8,2,3,128]{3,1,2,0:T(2,128)S(1)}, u32[]{:S(2)}, u32[]{:S(2)}) async-start(f32[8,2,3,128]{3,1,2,0:T(2,128)} %broadcast_in_dim.16), calls=%async_computation.5 | async-start | bytes 49152 | tf_op jit(solution)/shard_map/all_to_all | solution.py:37
  153.5 13.8 %partial_attention.3 = bf16[8,128,640]{2,1,0:T(8,128)(2,1)} custom-call(s32[12]{0:T(128)} %concatenate.17.meta_ref, bf16[8,136,512]{2,1,0:T(8,128)(2,1)} %copy-done.1, bf16[2,2,128,256]{3,2,1,0:T(8,128)(2,1)} %copy-done.2, bf16[2,2,128,256]{3,2,1,0:T(8,128)(2,1)} %copy-done.7, bf16[2,2,128,256]{3,2,1,0:T(8,128)(2,1)} %copy-done.9, ...), custom_call_target="tpu_custom_call", output_to_operand_aliasing={{}: (10, {})} | custom-call | flops 10000000000 | bytes 4000000 | tf_op jit(solution)/shard_map/partial_attention/pallas_call | solution.py:339
  167.3 5.1 %all-to-all-start.1 = ((bf16[8,128,640]{2,1,0:T(8,128)(2,1)}), bf16[8,128,640]{2,1,0:T(8,128)(2,1)S(1)}, u32[]{:S(2)}, u32[]{:S(2)}) async-start(bf16[8,128,640]{2,1,0:T(8,128)(2,1)} %partial_attention.3), calls=%async_computation.1 | async-start | bytes 2621440 | tf_op jit(solution)/shard_map/all_to_all | solution.py:481
  172.4 17.7 %all-to-all-done.1.parts_ref = bf16[8,128,640]{2,1,0:T(8,128)(2,1)S(1)} async-done(((bf16[8,128,640]{2,1,0:T(8,128)(2,1)}), bf16[8,128,640]{2,1,0:T(8,128)(2,1)S(1)}, u32[]{:S(2)}, u32[]{:S(2)}) %all-to-all-start.1) | async-done | bytes 1310752 | tf_op jit(solution)/shard_map/all_to_all | solution.py:481
  190.2 0.7 broadcast_in_dim.17
  190.9 4.5 %all-to-all-start.6 = ((f32[32,3,2,128]{3,2,1,0:T(2,128)}), f32[32,3,2,128]{3,2,1,0:T(2,128)S(1)}, u32[]{:S(2)}, u32[]{:S(2)}) async-start(f32[32,3,2,128]{3,2,1,0:T(2,128)} %broadcast_in_dim.17), calls=%async_computation.6 | async-start | bytes 196608 | tf_op jit(solution)/shard_map/all_to_all | solution.py:37
  195.4 3.2 %shard_map.139 = bf16[128,1024]{1,0:T(8,128)(2,1)} custom-call(bf16[8,128,640]{2,1,0:T(8,128)(2,1)} %copy-done), custom_call_target="tpu_custom_call" | custom-call | tf_op jit(solution)/shard_map/pallas_call | solution.py:397
  198.5 4.2 %all-to-all-done.6 = f32[32,3,2,128]{3,2,1,0:T(2,128)S(1)} async-done(((f32[32,3,2,128]{3,2,1,0:T(2,128)}), f32[32,3,2,128]{3,2,1,0:T(2,128)S(1)}, u32[]{:S(2)}, u32[]{:S(2)}) %all-to-all-start.6) | async-done | bytes 98336 | tf_op jit(solution)/shard_map/all_to_all | solution.py:37
  203.2 0.6 minimum_negate_fusion
  (91 shorter events, 2.8 us)
Async XLA Ops:
  0.6 45.3 %copy-start.16 = (s32[8]{0:T(128)S(1)}, s32[8]{0:T(128)}, u32[]{:S(2)}) copy-start(s32[8]{0:T(128)} %param.15) | copy-start | bytes 100
  1.5 6.9 %collective-permute-start.3 = (bf16[128,256]{1,0:T(8,128)(2,1)S(1)}, bf16[128,256]{1,0:T(8,128)(2,1)S(1)}, u32[]{:S(2)}, u32[]{:S(2)}) collective-permute-start(bf16[128,256]{1,0:T(8,128)(2,1)S(1)} %pad_maximum_fusion.3), channel_id=1, source_target_pairs={{0,34},{2,32},{4,102},{6,100},{8,170},{10,168},{12,238},{14,236},{... | collective-permute-start | bytes 196616 | tf_op jit(solution)/shard_map/ppermute | solution.py:459
  5.9 5.4 %collective-permute-start.2 = (bf16[128,256]{1,0:T(8,128)(2,1)S(1)}, bf16[128,256]{1,0:T(8,128)(2,1)S(1)}, u32[]{:S(2)}, u32[]{:S(2)}) collective-permute-start(bf16[128,256]{1,0:T(8,128)(2,1)S(1)} %pad_maximum_fusion.2), channel_id=1, source_target_pairs={{0,32},{2,34},{4,100},{6,102},{8,168},{10,170},{12,236},{14,238},{... | collective-permute-start | bytes 196616 | tf_op jit(solution)/shard_map/ppermute | solution.py:459
  7.7 3.6 %collective-permute-start.1 = (bf16[128,256]{1,0:T(8,128)(2,1)S(1)}, bf16[128,256]{1,0:T(8,128)(2,1)S(1)}, u32[]{:S(2)}, u32[]{:S(2)}) collective-permute-start(bf16[128,256]{1,0:T(8,128)(2,1)S(1)} %pad_maximum_fusion.3), channel_id=1, source_target_pairs={{0,2},{2,0},{4,70},{6,68},{8,138},{10,136},{12,206},{14,204},{16,1... | collective-permute-start | bytes 196616 | tf_op jit(solution)/shard_map/ppermute | solution.py:459
  7.7 3.6 %collective-permute-start = (bf16[128,256]{1,0:T(8,128)(2,1)S(1)}, bf16[128,256]{1,0:T(8,128)(2,1)S(1)}, u32[]{:S(2)}, u32[]{:S(2)}) collective-permute-start(bf16[128,256]{1,0:T(8,128)(2,1)S(1)} %pad_maximum_fusion.2), channel_id=1, source_target_pairs={{0,0},{2,2},{4,68},{6,70},{8,136},{10,138},{12,204},{14,206},{16,1... | collective-permute-start | bytes 196616 | tf_op jit(solution)/shard_map/ppermute | solution.py:459
  11.4 50.1 %copy-start.2 = (bf16[2,2,128,256]{3,2,1,0:T(8,128)(2,1)}, bf16[2,2,128,256]{3,2,1,0:T(8,128)(2,1)S(1)}, u32[]{:S(2)}) copy-start(bf16[2,2,128,256]{3,2,1,0:T(8,128)(2,1)S(1)} %pad_maximum_fusion.refs_0_) | copy-start | bytes 786436
  11.4 13.4 %collective-permute-start.8 = (bf16[2,2,128,256]{3,2,1,0:T(8,128)(2,1)S(1)}, bf16[2,2,128,256]{3,2,1,0:T(8,128)(2,1)S(1)}, u32[]{:S(2)}, u32[]{:S(2)}) collective-permute-start(bf16[2,2,128,256]{3,2,1,0:T(8,128)(2,1)S(1)} %pad_maximum_fusion.refs_0_), channel_id=1, source_target_pairs={{0,28},{4,0},{8,4},{12,8},{16,12},{20,16},{24,20},{28,24},{1,29},{... | collective-permute-start | bytes 786440 | tf_op jit(solution)/shard_map/ppermute | solution.py:465
  20.1 8.9 %collective-permute-start.4 = (bf16[2,2,128,256]{3,2,1,0:T(8,128)(2,1)S(1)}, bf16[2,2,128,256]{3,2,1,0:T(8,128)(2,1)S(1)}, u32[]{:S(2)}, u32[]{:S(2)}) collective-permute-start(bf16[2,2,128,256]{3,2,1,0:T(8,128)(2,1)S(1)} %pad_maximum_fusion.refs_0_), channel_id=1, source_target_pairs={{0,4},{4,8},{8,12},{12,16},{16,20},{20,24},{24,28},{28,0},{1,5},{5... | collective-permute-start | bytes 786440 | tf_op jit(solution)/shard_map/ppermute | solution.py:465
  24.8 36.7 %copy-start.6 = (bf16[2,2,128,256]{3,2,1,0:T(8,128)(2,1)}, bf16[2,2,128,256]{3,2,1,0:T(8,128)(2,1)S(1)}, u32[]{:S(2)}) copy-start(bf16[2,2,128,256]{3,2,1,0:T(8,128)(2,1)S(1)} %collective-permute-done.8.refs_7_) | copy-start | bytes 786436
  24.8 6.8 %collective-permute-start.9 = (bf16[2,2,128,256]{3,2,1,0:T(8,128)(2,1)S(1)}, bf16[2,2,128,256]{3,2,1,0:T(8,128)(2,1)S(1)}, u32[]{:S(2)}, u32[]{:S(2)}) collective-permute-start(bf16[2,2,128,256]{3,2,1,0:T(8,128)(2,1)S(1)} %collective-permute-done.8.refs_7_), channel_id=1, source_target_pairs={{0,28},{4,0},{8,4},{12,8},{16,12},{20,16},{24,20},{28,24},{1,29},{... | collective-permute-start | bytes 786440 | tf_op jit(solution)/shard_map/ppermute | solution.py:465
  29.0 32.6 %copy-start.7 = (bf16[2,2,128,256]{3,2,1,0:T(8,128)(2,1)}, bf16[2,2,128,256]{3,2,1,0:T(8,128)(2,1)S(1)}, u32[]{:S(2)}) copy-start(bf16[2,2,128,256]{3,2,1,0:T(8,128)(2,1)S(1)} %collective-permute-done.4.refs_1_) | copy-start | bytes 786436
  29.0 16.9 %collective-permute-start.5 = (bf16[2,2,128,256]{3,2,1,0:T(8,128)(2,1)S(1)}, bf16[2,2,128,256]{3,2,1,0:T(8,128)(2,1)S(1)}, u32[]{:S(2)}, u32[]{:S(2)}) collective-permute-start(bf16[2,2,128,256]{3,2,1,0:T(8,128)(2,1)S(1)} %collective-permute-done.4.refs_1_), channel_id=1, source_target_pairs={{0,4},{4,8},{8,12},{12,16},{16,20},{20,24},{24,28},{28,0},{1,5},{5... | collective-permute-start | bytes 786440 | tf_op jit(solution)/shard_map/ppermute | solution.py:465
  31.6 30.0 %copy-start.8 = (bf16[2,2,128,256]{3,2,1,0:T(8,128)(2,1)}, bf16[2,2,128,256]{3,2,1,0:T(8,128)(2,1)S(1)}, u32[]{:S(2)}) copy-start(bf16[2,2,128,256]{3,2,1,0:T(8,128)(2,1)S(1)} %collective-permute-done.9.refs_6_) | copy-start | bytes 786436
  31.6 14.6 %collective-permute-start.10 = (bf16[2,2,128,256]{3,2,1,0:T(8,128)(2,1)S(1)}, bf16[2,2,128,256]{3,2,1,0:T(8,128)(2,1)S(1)}, u32[]{:S(2)}, u32[]{:S(2)}) collective-permute-start(bf16[2,2,128,256]{3,2,1,0:T(8,128)(2,1)S(1)} %collective-permute-done.9.refs_6_), channel_id=1, source_target_pairs={{0,28},{4,0},{8,4},{12,8},{16,12},{20,16},{24,20},{28,24},{1,29},{... | collective-permute-start | bytes 786440 | tf_op jit(solution)/shard_map/ppermute | solution.py:465
  36.8 24.7 %all-to-all-start = ((bf16[8,136,512]{2,1,0:T(8,128)(2,1)}), bf16[8,136,512]{2,1,0:T(8,128)(2,1)S(1)}, u32[]{:S(2)}, u32[]{:S(2)}) async-start(bf16[8,136,512]{2,1,0:T(8,128)(2,1)} %queries_to_send.1), calls=%async_computation | async-start | bytes 2228224 | tf_op jit(solution)/shard_map/all_to_all | solution.py:475
  45.9 15.7 %copy-start.9 = (bf16[2,2,128,256]{3,2,1,0:T(8,128)(2,1)}, bf16[2,2,128,256]{3,2,1,0:T(8,128)(2,1)S(1)}, u32[]{:S(2)}) copy-start(bf16[2,2,128,256]{3,2,1,0:T(8,128)(2,1)S(1)} %collective-permute-done.5.refs_2_) | copy-start | bytes 786436
  45.9 9.1 %collective-permute-start.6 = (bf16[2,2,128,256]{3,2,1,0:T(8,128)(2,1)S(1)}, bf16[2,2,128,256]{3,2,1,0:T(8,128)(2,1)S(1)}, u32[]{:S(2)}, u32[]{:S(2)}) collective-permute-start(bf16[2,2,128,256]{3,2,1,0:T(8,128)(2,1)S(1)} %collective-permute-done.5.refs_2_), channel_id=1, source_target_pairs={{0,4},{4,8},{8,12},{12,16},{16,20},{20,24},{24,28},{28,0},{1,5},{5... | collective-permute-start | bytes 786440 | tf_op jit(solution)/shard_map/ppermute | solution.py:465
  46.2 15.4 %copy-start.3 = (bf16[2,2,128,256]{3,2,1,0:T(8,128)(2,1)}, bf16[2,2,128,256]{3,2,1,0:T(8,128)(2,1)S(1)}, u32[]{:S(2)}) copy-start(bf16[2,2,128,256]{3,2,1,0:T(8,128)(2,1)S(1)} %collective-permute-done.10.refs_5_) | copy-start | bytes 786436
  46.2 9.6 %collective-permute-start.11 = (bf16[2,128,256]{2,1,0:T(8,128)(2,1)S(1)}, bf16[2,128,256]{2,1,0:T(8,128)(2,1)S(1)}, u32[]{:S(2)}, u32[]{:S(2)}) collective-permute-start(bf16[2,128,256]{2,1,0:T(8,128)(2,1)S(1)} %slice_bitcast_fusion), channel_id=1, source_target_pairs={{0,28},{4,0},{8,4},{12,8},{16,12},{20,16},{24,20},{28,24},{1,29},{... | collective-permute-start | bytes 393224 | tf_op jit(solution)/shard_map/ppermute | solution.py:465
  55.0 6.6 %copy-start.4 = (bf16[2,2,128,256]{3,2,1,0:T(8,128)(2,1)}, bf16[2,2,128,256]{3,2,1,0:T(8,128)(2,1)S(1)}, u32[]{:S(2)}) copy-start(bf16[2,2,128,256]{3,2,1,0:T(8,128)(2,1)S(1)} %collective-permute-done.6.refs_3_) | copy-start | bytes 786436
  55.0 5.5 %collective-permute-start.7 = (bf16[2,128,256]{2,1,0:T(8,128)(2,1)S(1)}, bf16[2,128,256]{2,1,0:T(8,128)(2,1)S(1)}, u32[]{:S(2)}, u32[]{:S(2)}) collective-permute-start(bf16[2,128,256]{2,1,0:T(8,128)(2,1)S(1)} %slice_bitcast_fusion.1), channel_id=1, source_target_pairs={{0,4},{4,8},{8,12},{12,16},{16,20},{20,24},{24,28},{28,0},{1,5},{5... | collective-permute-start | bytes 393224 | tf_op jit(solution)/shard_map/ppermute | solution.py:465
  61.6 1.0 copy-start.1
  69.9 10.7 %all-to-all-start.2 = ((bf16[8,8,640]{2,1,0:T(8,128)(2,1)}), bf16[8,8,640]{2,1,0:T(8,128)(2,1)S(1)}, u32[]{:S(2)}, u32[]{:S(2)}) async-start(bf16[8,8,640]{2,1,0:T(8,128)(2,1)} %chosen_attention.1), calls=%async_computation.2 | async-start | bytes 163840 | tf_op jit(solution)/shard_map/all_to_all | solution.py:477
  80.6 0.6 copy-start.5
  82.9 4.6 %copy-start.10 = (bf16[4,2048]{1,0:T(4,128)(2,1)S(1)}, bf16[4,2048]{1,0:T(4,128)(2,1)}, u32[]{:S(2)}) copy-start(bf16[4,2048]{1,0:T(4,128)(2,1)} %param.17) | copy-start | bytes 49156
  82.9 7.7 %copy-start.12 = (f32[2048]{0:T(1024)S(1)}, f32[2048]{0:T(1024)}, u32[]{:S(2)}) copy-start(f32[2048]{0:T(1024)} %param.18) | copy-start | bytes 24580
  87.5 20.7 %copy-start.13 = (s32[512]{0:T(512)S(1)}, s32[512]{0:T(512)}, u32[]{:S(2)}) copy-start(s32[512]{0:T(512)} %param.21) | copy-start | bytes 6148
  87.6 2.9 %collective-permute-start.12 = (bf16[4,4096]{1,0:T(4,128)(2,1)S(1)}, bf16[4,4096]{1,0:T(4,128)(2,1)S(1)}, u32[]{:S(2)}, u32[]{:S(2)}) collective-permute-start(bf16[4,4096]{1,0:T(4,128)(2,1)S(1)} %convert_element_type.25), channel_id=1, source_target_pairs={{0,1},{1,0},{2,3},{3,2},{4,5},{5,4},{6,7},{7,6},{8,9},{9,8},{10,11... | collective-permute-start | bytes 98312 | tf_op jit(solution)/shard_map/ppermute | solution.py:43
  104.7 14.9 %all-to-all-start.4 = ((bf16[4,16,4,2048]{3,2,1,0:T(4,128)(2,1)}), bf16[4,16,4,2048]{3,2,1,0:T(4,128)(2,1)S(1)}, u32[]{:S(2)}, u32[]{:S(2)}) async-start(bf16[4,16,4,2048]{3,2,1,0:T(4,128)(2,1)} %broadcast_in_dim.14), calls=%async_computation.4 | async-start | bytes 2097152 | tf_op jit(solution)/shard_map/all_to_all | solution.py:37
  119.9 16.3 %collective-permute-start.14 = (bf16[256,2048]{1,0:T(8,128)(2,1)S(1)}, bf16[256,2048]{1,0:T(8,128)(2,1)}, u32[]{:S(2)}, u32[]{:S(2)}) collective-permute-start(bf16[256,2048]{1,0:T(8,128)(2,1)S(1)} %reshape.115), channel_id=1, source_target_pairs={{0,2},{2,0},{1,3},{3,1},{4,6},{6,4},{5,7},{7,5},{8,10},{10,8},{9,1... | collective-permute-start | bytes 3145736 | tf_op jit(solution)/shard_map/ppermute | solution.py:500
  128.2 7.9 %collective-permute-start.13 = (bf16[128,1002]{0,1:T(8,128)(2,1)S(1)}, bf16[128,1002]{0,1:T(8,128)(2,1)S(1)}, u32[]{:S(2)}, u32[]{:S(2)}) collective-permute-start(bf16[128,1002]{0,1:T(8,128)(2,1)S(1)} %dynamic-slice_convert_fusion.1), channel_id=1, source_target_pairs={{0,1},{1,0},{2,3},{3,2},{4,5},{5,4},{6,7},{7,6},{8,9},{9,8},{10,11... | collective-permute-start | bytes 769544 | tf_op jit(solution)/shard_map/ppermute | solution.py:43
  140.0 7.0 %collective-permute-start.15 = (bf16[128,1002]{0,1:T(8,128)(2,1)S(1)}, bf16[128,1002]{0,1:T(8,128)(2,1)S(1)}, u32[]{:S(2)}, u32[]{:S(2)}) collective-permute-start(bf16[128,1002]{0,1:T(8,128)(2,1)S(1)} %dynamic-slice_convert_fusion), channel_id=1, source_target_pairs={{0,1},{1,0},{2,3},{3,2},{4,5},{5,4},{6,7},{7,6},{8,9},{9,8},{10,11... | collective-permute-start | bytes 769544 | tf_op jit(solution)/shard_map/ppermute | solution.py:43
  148.1 19.2 %all-to-all-start.5 = ((f32[8,2,3,128]{3,1,2,0:T(2,128)}), f32[8,2,3,128]{3,1,2,0:T(2,128)S(1)}, u32[]{:S(2)}, u32[]{:S(2)}) async-start(f32[8,2,3,128]{3,1,2,0:T(2,128)} %broadcast_in_dim.16), calls=%async_computation.5 | async-start | bytes 49152 | tf_op jit(solution)/shard_map/all_to_all | solution.py:37
  167.3 35.9 %copy-start.14 = (f32[512]{0:T(512)S(1)}, f32[512]{0:T(512)}, u32[]{:S(2)}) copy-start(f32[512]{0:T(512)} %param.23) | copy-start | bytes 6148
  167.3 35.9 %copy-start.15 = (f32[512]{0:T(512)S(1)}, f32[512]{0:T(512)}, u32[]{:S(2)}) copy-start(f32[512]{0:T(512)} %param.22) | copy-start | bytes 6148
  167.3 22.9 %all-to-all-start.1 = ((bf16[8,128,640]{2,1,0:T(8,128)(2,1)}), bf16[8,128,640]{2,1,0:T(8,128)(2,1)S(1)}, u32[]{:S(2)}, u32[]{:S(2)}) async-start(bf16[8,128,640]{2,1,0:T(8,128)(2,1)} %partial_attention.3), calls=%async_computation.1 | async-start | bytes 2621440 | tf_op jit(solution)/shard_map/all_to_all | solution.py:481
  190.2 5.2 %copy-start = (bf16[8,128,640]{2,1,0:T(8,128)(2,1)}, bf16[8,128,640]{2,1,0:T(8,128)(2,1)S(1)}, u32[]{:S(2)}) copy-start(bf16[8,128,640]{2,1,0:T(8,128)(2,1)S(1)} %all-to-all-done.1.parts_ref) | copy-start | bytes 3932164
  190.9 11.9 %all-to-all-start.6 = ((f32[32,3,2,128]{3,2,1,0:T(2,128)}), f32[32,3,2,128]{3,2,1,0:T(2,128)S(1)}, u32[]{:S(2)}, u32[]{:S(2)}) async-start(f32[32,3,2,128]{3,2,1,0:T(2,128)} %broadcast_in_dim.17), calls=%async_computation.6 | async-start | bytes 196608 | tf_op jit(solution)/shard_map/all_to_all | solution.py:37
  203.2 0.6 copy-start.11
where the time goes:
time: 206 us; the launch traced here: 204 us
  waiting for transfers between devices  68.4 us (33%)
  starting transfers between devices  64.8 us (31%)
  Pallas kernels  35.5 us (17%)
  blocking collectives  12.4 us (6%)
  matrix products  11.9 us (6%)
  local copies, waits for them, and re-layouts  6.96 us (3%)
  other arithmetic  2.78 us (1%)
    pallas_call x2, Pallas kernels, partial_attention(): pl.pallas_call(functools.partial(attention_kernel, first), grid_spec=pltp...  21.2 us
    ppermute x8, waiting for transfers between devices, shifted(): return lax.ppermute(a, 'ctx_2', [(k, (k + d) % nz) for k in range(nz)])  18.8 us
    ppermute x8, starting transfers between devices, shifted(): return lax.ppermute(a, 'ctx_2', [(k, (k + d) % nz) for k in range(nz)])  18.2 us
    all_to_all x1, waiting for transfers between devices, per_device(): arrived = lax.all_to_all(parts, XC, 0, 0, tiled=True)  17.7 us
    all_to_all x3, waiting for transfers between devices, spread(): lax.all_to_all(jnp.broadcast_to(shard[None], (n, *shard.shape)), axes, 0,...  15.3 us
    all_to_all x3, starting transfers between devices, spread(): lax.all_to_all(jnp.broadcast_to(shard[None], (n, *shard.shape)), axes, 0,...  13.4 us
    all_to_all x1, blocking collectives, spread(): lax.all_to_all(jnp.broadcast_to(shard[None], (n, *shard.shape)), axes, 0,...  12.4 us
    all_to_all x1, starting transfers between devices, per_device(): q_all = lax.all_to_all(q_send, XC, 0, 0, tiled=True)  9.04 us
  transfers between devices with their start and end apart: 22, of which 13 were waited for; matrix products, arithmetic and copies ran while one was open for 3% of the time, Pallas kernels for 13%

commit v1 on v0

--- a/solution.py
+++ b/solution.py
@@ -423,6 +423,7 @@
     old_logp,
     advantage,
 ):
+    tok_rows = queries.shape[0]
     count = scored.shape[0]
     nx, ny, nz, cores = [lax.axis_size(a) for a in CTX]
     x, y, z, core = [lax.axis_index(a) for a in CTX]
@@ -454,30 +455,29 @@
         ]
 
     mine, others = of_head(core), of_head(1 - core)
-    own = jnp.stack(
-        [
-            jnp.stack([lax.ppermute(mine, CTX, handed(dy, 0)), lax.ppermute(others, CTX, handed(dy, 1))])
-            for dy in range(ny)
-        ]
-    )
+    pieces = []
+    for dy in range(ny):
+        for dc in range(cores):
+            pieces.append(lax.ppermute(others if dc else mine, CTX, handed(dy, dc)))
+    own = jnp.stack(pieces).reshape(ny, cores, tok_rows, 2 * HEAD_SIZE)
 
     def shifted(a, d):
         return lax.ppermute(a, "ctx_2", [(k, (k + d) % nz) for k in range(nz)])
 
+    far = nz // 2
     kv_all = [own] + [None] * (nz - 1)
-    for d in range(1, nz // 2):
+    for d in range(1, far):
         kv_all[d] = shifted(kv_all[d - 1], 1)
         kv_all[nz - d] = shifted(kv_all[(nz - d + 1) % nz], -1)
-    far = nz // 2
     kv_all[far] = jnp.stack([shifted(kv_all[far - 1][0], 1), shifted(kv_all[far + 1][1], -1)])
-
     q_send = queries_to_send(scored, queries, nx)
     q_all = lax.all_to_all(q_send, XC, 0, 0, tiled=True)
     few = chosen_attention(meta, q_all, kv_all)
     few = lax.all_to_all(few, XC, 0, 0, tiled=True)
     chosen = merged_attention(few)
-    parts = partial_attention(meta, q_all, kv_all, 0, nx // 2, q_all)
-    parts = partial_attention(meta, q_all, kv_all, nx // 2, nx - nx // 2, parts)
+    parts = q_all
+    for n in range(nx):
+        parts = partial_attention(meta, q_all, kv_all, n, 1, parts)
     arrived = lax.all_to_all(parts, XC, 0, 0, tiled=True)
     attended = merged_attention(arrived)
 

time: 206 us -> 203 us (0.985)
  blocking collectives: 12.4 us -> 0 us
  Pallas kernels: 35.5 us -> 42.3 us
  starting transfers between devices: 64.8 us -> 71.4 us
  waiting for transfers between devices: 68.4 us -> 65 us
    all_to_all x1 -> x0, blocking collectives: 12.4 us -> none  [spread(): lax.all_to_all(jnp.broadcast_to(shard[None], (n, *shard.shape)), axes, 0,...]
    pallas_call x2 -> x4, Pallas kernels: 21.2 us -> 28 us  [partial_attention(): pl.pallas_call(functools.partial(attention_kernel, first), grid_spec=pltp...]
    all_to_all x3 -> x4, starting transfers between devices: 13.4 us -> 18.4 us  [spread(): lax.all_to_all(jnp.broadcast_to(shard[None], (n, *shard.shape)), axes, 0,...]
    all_to_all x3 -> x4, waiting for transfers between devices: 15.3 us -> 13.6 us  [spread(): lax.all_to_all(jnp.broadcast_to(shard[None], (n, *shard.shape)), axes, 0,...]
  transfers between devices with their start and end apart: 22 -> 23, of which waited for: 13 -> 15; matrix products, arithmetic and copies ran while one was open for 3% -> 3% of each run, Pallas kernels for 13% -> 16%
where the time goes in v1:
time: 203 us; the launch traced here: 202 us
  starting transfers between devices  71.4 us (35%)
  waiting for transfers between devices  65 us (32%)
  Pallas kernels  42.3 us (21%)
  matrix products  11.9 us (6%)
  local copies, waits for them, and re-layouts  7.68 us (4%)
  other arithmetic  2.75 us (1%)
    pallas_call x4, Pallas kernels, partial_attention(): pl.pallas_call(functools.partial(attention_kernel, first), grid_spec=pltp...  28 us
    ppermute x8, starting transfers between devices, shifted(): return lax.ppermute(a, 'ctx_2', [(k, (k + d) % nz) for k in range(nz)])  18.7 us
    all_to_all x4, starting transfers between devices, spread(): lax.all_to_all(jnp.broadcast_to(shard[None], (n, *shard.shape)), axes, 0,...  18.4 us
    ppermute x8, waiting for transfers between devices, shifted(): return lax.ppermute(a, 'ctx_2', [(k, (k + d) % nz) for k in range(nz)])  18.2 us
    all_to_all x1, waiting for transfers between devices, per_device(): arrived = lax.all_to_all(parts, XC, 0, 0, tiled=True)  17.7 us
    all_to_all x4, waiting for transfers between devices, spread(): lax.all_to_all(jnp.broadcast_to(shard[None], (n, *shard.shape)), axes, 0,...  13.6 us
    all_to_all x1, starting transfers between devices, per_device(): q_all = lax.all_to_all(q_send, XC, 0, 0, tiled=True)  9.88 us
    ppermute x3, waiting for transfers between devices, swap_heads(): return lax.ppermute(shard, 'head', [(0, 1), (1, 0)])  8.11 us
  transfers between devices with their start and end apart: 23, of which 15 were waited for; matrix products, arithmetic and copies ran while one was open for 3% of the time, Pallas kernels for 16%

profile of v1, /device:TPU:1, one launch (start us, length us, event | category | flops | bytes accessed | tf_op | source)
XLA Modules:
  0.0 202.2 jit_solution(14870244033272161703)
XLA Ops:
  0.6 0.8 constant_dynamic-slice_fusion.5
  1.5 4.4 %collective-permute-start.3 = (bf16[128,256]{1,0:T(8,128)(2,1)S(1)}, bf16[128,256]{1,0:T(8,128)(2,1)S(1)}, u32[]{:S(2)}, u32[]{:S(2)}) collective-permute-start(bf16[128,256]{1,0:T(8,128)(2,1)S(1)} %pad_maximum_fusion.3), channel_id=1, source_target_pairs={{0,34},{2,32},{4,102},{6,100},{8,170},{10,168},{12,238},{14,236},{... | collective-permute-start | bytes 196616 | tf_op jit(solution)/shard_map/ppermute | solution.py:461
  5.9 1.9 collective-permute-start.2
  7.7 0.7 collective-permute-start
  8.4 2.2 %collective-permute-done.2 = bf16[128,256]{1,0:T(8,128)(2,1)S(1)} collective-permute-done((bf16[128,256]{1,0:T(8,128)(2,1)S(1)}, bf16[128,256]{1,0:T(8,128)(2,1)S(1)}, u32[]{:S(2)}, u32[]{:S(2)}) %collective-permute-start.2) | collective-permute-done | bytes 65568 | tf_op jit(solution)/shard_map/ppermute | solution.py:461
  10.7 9.2 %collective-permute-start.8 = (bf16[2,2,128,256]{3,2,1,0:T(8,128)(2,1)S(1)}, bf16[2,2,128,256]{3,2,1,0:T(8,128)(2,1)S(1)}, u32[]{:S(2)}, u32[]{:S(2)}) collective-permute-start(bf16[2,2,128,256]{3,2,1,0:T(8,128)(2,1)S(1)} %bitcast.70), channel_id=1, source_target_pairs={{0,28},{4,0},{8,4},{12,8},{16,12},{20,16},{24,20},{28,24},{1,29},{... | collective-permute-start | bytes 786440 | tf_op jit(solution)/shard_map/ppermute | solution.py:465
  19.9 4.1 %collective-permute-done.8.refs_7_ = bf16[2,2,128,256]{3,2,1,0:T(8,128)(2,1)S(1)} collective-permute-done((bf16[2,2,128,256]{3,2,1,0:T(8,128)(2,1)S(1)}, bf16[2,2,128,256]{3,2,1,0:T(8,128)(2,1)S(1)}, u32[]{:S(2)}, u32[]{:S(2)}) %collective-permute-start.8) | collective-permute-done | bytes 262176 | tf_op jit(solution)/shard_map/ppermute | solution.py:465
  23.9 3.5 %collective-permute-start.9 = (bf16[2,2,128,256]{3,2,1,0:T(8,128)(2,1)S(1)}, bf16[2,2,128,256]{3,2,1,0:T(8,128)(2,1)S(1)}, u32[]{:S(2)}, u32[]{:S(2)}) collective-permute-start(bf16[2,2,128,256]{3,2,1,0:T(8,128)(2,1)S(1)} %collective-permute-done.8.refs_7_), channel_id=1, source_target_pairs={{0,28},{4,0},{8,4},{12,8},{16,12},{20,16},{24,20},{28,24},{1,29},{... | collective-permute-start | bytes 786440 | tf_op jit(solution)/shard_map/ppermute | solution.py:465
  27.4 0.7 collective-permute-done.4.refs_1_
  28.1 2.6 %collective-permute-done.9.refs_6_ = bf16[2,2,128,256]{3,2,1,0:T(8,128)(2,1)S(1)} collective-permute-done((bf16[2,2,128,256]{3,2,1,0:T(8,128)(2,1)S(1)}, bf16[2,2,128,256]{3,2,1,0:T(8,128)(2,1)S(1)}, u32[]{:S(2)}, u32[]{:S(2)}) %collective-permute-start.9) | collective-permute-done | bytes 262176 | tf_op jit(solution)/shard_map/ppermute | solution.py:465
  30.7 3.1 %collective-permute-start.10 = (bf16[2,2,128,256]{3,2,1,0:T(8,128)(2,1)S(1)}, bf16[2,2,128,256]{3,2,1,0:T(8,128)(2,1)S(1)}, u32[]{:S(2)}, u32[]{:S(2)}) collective-permute-start(bf16[2,2,128,256]{3,2,1,0:T(8,128)(2,1)S(1)} %collective-permute-done.9.refs_6_), channel_id=1, source_target_pairs={{0,28},{4,0},{8,4},{12,8},{16,12},{20,16},{24,20},{28,24},{1,29},{... | collective-permute-start | bytes 786440 | tf_op jit(solution)/shard_map/ppermute | solution.py:465
  33.8 2.1 %queries_to_send.1 = bf16[8,136,512]{2,1,0:T(8,128)(2,1)} custom-call(s32[4]{0:T(128)} %scored_ref.1, bf16[128,1024]{1,0:T(8,128)(2,1)} %q_ref.1), custom_call_target="tpu_custom_call" | custom-call | tf_op jit(solution)/shard_map/queries_to_send/pallas_call | solution.py:114
  36.0 9.9 %all-to-all-start = ((bf16[8,136,512]{2,1,0:T(8,128)(2,1)}), bf16[8,136,512]{2,1,0:T(8,128)(2,1)S(1)}, u32[]{:S(2)}, u32[]{:S(2)}) async-start(bf16[8,136,512]{2,1,0:T(8,128)(2,1)} %queries_to_send.1), calls=%async_computation | async-start | bytes 2228224 | tf_op jit(solution)/shard_map/all_to_all | solution.py:474
  46.2 2.7 %collective-permute-start.11 = (bf16[2,128,256]{2,1,0:T(8,128)(2,1)S(1)}, bf16[2,128,256]{2,1,0:T(8,128)(2,1)S(1)}, u32[]{:S(2)}, u32[]{:S(2)}) collective-permute-start(bf16[2,128,256]{2,1,0:T(8,128)(2,1)S(1)} %slice_bitcast_fusion), channel_id=1, source_target_pairs={{0,28},{4,0},{8,4},{12,8},{16,12},{20,16},{24,20},{28,24},{1,29},{... | collective-permute-start | bytes 393224 | tf_op jit(solution)/shard_map/ppermute | solution.py:465
  48.9 6.1 %collective-permute-done.6.refs_3_ = bf16[2,2,128,256]{3,2,1,0:T(8,128)(2,1)S(1)} collective-permute-done((bf16[2,2,128,256]{3,2,1,0:T(8,128)(2,1)S(1)}, bf16[2,2,128,256]{3,2,1,0:T(8,128)(2,1)S(1)}, u32[]{:S(2)}, u32[]{:S(2)}) %collective-permute-start.6) | collective-permute-done | bytes 262176 | tf_op jit(solution)/shard_map/ppermute | solution.py:465
  55.1 0.6 concatenate.17.meta_ref
  55.7 4.7 %collective-permute-done.7 = bf16[2,128,256]{2,1,0:T(8,128)(2,1)S(1)} collective-permute-done((bf16[2,128,256]{2,1,0:T(8,128)(2,1)S(1)}, bf16[2,128,256]{2,1,0:T(8,128)(2,1)S(1)}, u32[]{:S(2)}, u32[]{:S(2)}) %collective-permute-start.7) | collective-permute-done | bytes 131104 | tf_op jit(solution)/shard_map/ppermute | solution.py:465
  60.5 0.7 pad_maximum_fusion.1.refs_4_
  61.6 1.0 copy-done.1
  62.6 7.3 %chosen_attention.1 = bf16[8,8,640]{2,1,0:T(8,128)(2,1)} custom-call(s32[12]{0:T(128)} %concatenate.17.meta_ref, bf16[8,136,512]{2,1,0:T(8,128)(2,1)} %copy-done.1, bf16[2,2,128,256]{3,2,1,0:T(8,128)(2,1)} %bitcast.72, bf16[2,2,128,256]{3,2,1,0:T(8,128)(2,1)} %copy-done.7, bf16[2,2,128,256]{3,2,1,0:T(8,128)(2,1)} %copy-done.9, ...), custom_call_target="tpu_custom_call" | custom-call | tf_op jit(solution)/shard_map/chosen_attention/pallas_call | solution.py:212
  69.9 5.8 %all-to-all-start.2 = ((bf16[8,8,640]{2,1,0:T(8,128)(2,1)}), bf16[8,8,640]{2,1,0:T(8,128)(2,1)S(1)}, u32[]{:S(2)}, u32[]{:S(2)}) async-start(bf16[8,8,640]{2,1,0:T(8,128)(2,1)} %chosen_attention.1), calls=%async_computation.2 | async-start | bytes 163840 | tf_op jit(solution)/shard_map/all_to_all | solution.py:476
  75.6 4.9 %all-to-all-done.2.parts_ref = bf16[8,8,640]{2,1,0:T(8,128)(2,1)S(1)} async-done(((bf16[8,8,640]{2,1,0:T(8,128)(2,1)}), bf16[8,8,640]{2,1,0:T(8,128)(2,1)S(1)}, u32[]{:S(2)}, u32[]{:S(2)}) %all-to-all-start.2) | async-done | bytes 81952 | tf_op jit(solution)/shard_map/all_to_all | solution.py:476
  80.6 0.6 copy-done.5
  81.2 1.7 shard_map.140
  82.9 4.6 %fusion.8 = f32[4,4096]{1,0:T(4,128)S(1)} fusion(bf16[1024,4096]{1,0:T(8,128)(2,1)} %param.19, bf16[8,1024]{1,0:T(8,128)(2,1)} %shard_map.140), kind=kOutput, calls=%fused_computation.33 | convolution fusion | flops 33554432 | bytes 8462336 | tf_op jit(solution)/shard_map/dot_general | solution.py:486
  87.7 2.8 %collective-permute-done.12 = bf16[4,4096]{1,0:T(4,128)(2,1)S(1)} collective-permute-done((bf16[4,4096]{1,0:T(4,128)(2,1)S(1)}, bf16[4,4096]{1,0:T(4,128)(2,1)S(1)}, u32[]{:S(2)}, u32[]{:S(2)}) %collective-permute-start.12) | collective-permute-done | bytes 32800 | tf_op jit(solution)/shard_map/ppermute | solution.py:43
  90.7 0.8 broadcast_in_dim.12
  91.5 3.7 %all-to-all-start.3 = ((bf16[16,4,2048]{2,1,0:T(4,128)(2,1)}), bf16[16,4,2048]{2,1,0:T(4,128)(2,1)S(1)}, u32[]{:S(2)}, u32[]{:S(2)}) async-start(bf16[16,4,2048]{2,1,0:T(4,128)(2,1)} %broadcast_in_dim.12), calls=%async_computation.3 | async-start | bytes 524288 | tf_op jit(solution)/shard_map/all_to_all | solution.py:37
  95.6 8.9 %all-to-all-done.3 = bf16[16,4,2048]{2,1,0:T(4,128)(2,1)S(1)} async-done(((bf16[16,4,2048]{2,1,0:T(4,128)(2,1)}), bf16[16,4,2048]{2,1,0:T(4,128)(2,1)S(1)}, u32[]{:S(2)}, u32[]{:S(2)}) %all-to-all-start.3) | async-done | bytes 262176 | tf_op jit(solution)/shard_map/all_to_all | solution.py:37
  104.5 1.5 broadcast_in_dim.14
  106.0 3.5 %all-to-all-start.4 = ((bf16[4,16,4,2048]{3,2,1,0:T(4,128)(2,1)}), bf16[4,16,4,2048]{3,2,1,0:T(4,128)(2,1)S(1)}, u32[]{:S(2)}, u32[]{:S(2)}) async-start(bf16[4,16,4,2048]{3,2,1,0:T(4,128)(2,1)} %broadcast_in_dim.14), calls=%async_computation.4 | async-start | bytes 2097152 | tf_op jit(solution)/shard_map/all_to_all | solution.py:37
  109.5 4.9 %partial_attention.4.refs_8_ = bf16[8,128,640]{2,1,0:T(8,128)(2,1)} custom-call(s32[12]{0:T(128)} %concatenate.17.meta_ref, bf16[8,136,512]{2,1,0:T(8,128)(2,1)} %copy-done.1, bf16[2,2,128,256]{3,2,1,0:T(8,128)(2,1)} %bitcast.73, bf16[2,2,128,256]{3,2,1,0:T(8,128)(2,1)} %copy-done.7, bf16[2,2,128,256]{3,2,1,0:T(8,128)(2,1)} %copy-done.9, ...), custom_call_target="tpu_custom_call" | custom-call | flops 5000000000 | bytes 4000000 | tf_op jit(solution)/shard_map/partial_attention/pallas_call | solution.py:339
  114.4 5.8 %partial_attention.5.refs_8_ = bf16[8,128,640]{2,1,0:T(8,128)(2,1)} custom-call(s32[12]{0:T(128)} %concatenate.17.meta_ref, bf16[8,136,512]{2,1,0:T(8,128)(2,1)} %copy-done.1, bf16[2,2,128,256]{3,2,1,0:T(8,128)(2,1)} %bitcast.74, bf16[2,2,128,256]{3,2,1,0:T(8,128)(2,1)} %copy-done.7, ...), custom_call_target="tpu_custom_call", output_to_operand_aliasing={{}: (10, {})} | custom-call | flops 5000000000 | bytes 4000000 | tf_op jit(solution)/shard_map/partial_attention/pallas_call | solution.py:339
  121.1 4.7 %collective-permute-start.14 = (bf16[256,2048]{1,0:T(8,128)(2,1)S(1)}, bf16[256,2048]{1,0:T(8,128)(2,1)}, u32[]{:S(2)}, u32[]{:S(2)}) collective-permute-start(bf16[256,2048]{1,0:T(8,128)(2,1)S(1)} %reshape.119), channel_id=1, source_target_pairs={{0,2},{2,0},{1,3},{3,1},{4,6},{6,4},{5,7},{7,5},{8,10},{10,8},{9,1... | collective-permute-start | bytes 3145736 | tf_op jit(solution)/shard_map/ppermute | solution.py:500
  125.9 3.5 %fusion.15 = f32[256,1002]{0,1:T(8,128)S(1)} fusion(bf16[256,2048]{1,0:T(8,128)(2,1)S(1)} %reshape.119, bf16[2048,1002]{0,1:T(8,128)(2,1)} %param.20), kind=kOutput, calls=%fused_computation.58 | convolution fusion | flops 1050673152 | bytes 6178816 | tf_op jit(solution)/shard_map/dot_general | solution.py:509
  129.5 7.7 %partial_attention.6.refs_8_ = bf16[8,128,640]{2,1,0:T(8,128)(2,1)} custom-call(s32[12]{0:T(128)} %concatenate.17.meta_ref, bf16[8,136,512]{2,1,0:T(8,128)(2,1)} %copy-done.1, bf16[2,2,128,256]{3,2,1,0:T(8,128)(2,1)} %bitcast.75, bf16[2,2,128,256]{3,2,1,0:T(8,128)(2,1)} %copy-done.7, ...), custom_call_target="tpu_custom_call", output_to_operand_aliasing={{}: (10, {})} | custom-call | flops 5000000000 | bytes 4000000 | tf_op jit(solution)/shard_map/partial_attention/pallas_call | solution.py:339
  137.4 3.8 %fusion.16 = f32[256,1002]{0,1:T(8,128)S(1)} fusion(bf16[256,2048]{1,0:T(8,128)(2,1)} %collective-permute-done.14, bf16[2048,1002]{0,1:T(8,128)(2,1)} %param.20), kind=kOutput, calls=%fused_computation.59 | convolution fusion | flops 1050673152 | bytes 6178816 | tf_op jit(solution)/shard_map/dot_general | solution.py:509
  141.2 1.7 collective-permute-start.15
  143.1 5.3 %collective-permute-done.15 = bf16[128,1002]{0,1:T(8,128)(2,1)S(1)} collective-permute-done((bf16[128,1002]{0,1:T(8,128)(2,1)S(1)}, bf16[128,1002]{0,1:T(8,128)(2,1)S(1)}, u32[]{:S(2)}, u32[]{:S(2)}) %collective-permute-start.15) | collective-permute-done | bytes 256544 | tf_op jit(solution)/shard_map/ppermute | solution.py:43
  148.8 0.6 broadcast_in_dim.16
  149.4 6.2 %all-to-all-start.5 = ((f32[8,2,3,128]{3,1,2,0:T(2,128)}), f32[8,2,3,128]{3,1,2,0:T(2,128)S(1)}, u32[]{:S(2)}, u32[]{:S(2)}) async-start(f32[8,2,3,128]{3,1,2,0:T(2,128)} %broadcast_in_dim.16), calls=%async_computation.5 | async-start | bytes 49152 | tf_op jit(solution)/shard_map/all_to_all | solution.py:37
  155.6 9.5 %partial_attention.7 = bf16[8,128,640]{2,1,0:T(8,128)(2,1)} custom-call(s32[12]{0:T(128)} %concatenate.17.meta_ref, bf16[8,136,512]{2,1,0:T(8,128)(2,1)} %copy-done.1, bf16[2,2,128,256]{3,2,1,0:T(8,128)(2,1)} %bitcast.76, bf16[2,2,128,256]{3,2,1,0:T(8,128)(2,1)} %copy-done.7, bf16[2,2,128,256]{3,2,1,0:T(8,128)(2,1)} %copy-done.9, ...), custom_call_target="tpu_custom_call", output_to_operand_aliasing={{}: (10, {})} | custom-call | flops 5000000000 | bytes 4000000 | tf_op jit(solution)/shard_map/partial_attention/pallas_call | solution.py:339
  165.1 5.1 %all-to-all-start.1 = ((bf16[8,128,640]{2,1,0:T(8,128)(2,1)}), bf16[8,128,640]{2,1,0:T(8,128)(2,1)S(1)}, u32[]{:S(2)}, u32[]{:S(2)}) async-start(bf16[8,128,640]{2,1,0:T(8,128)(2,1)} %partial_attention.7), calls=%async_computation.1 | async-start | bytes 2621440 | tf_op jit(solution)/shard_map/all_to_all | solution.py:481
  170.3 17.7 %all-to-all-done.1.parts_ref = bf16[8,128,640]{2,1,0:T(8,128)(2,1)S(1)} async-done(((bf16[8,128,640]{2,1,0:T(8,128)(2,1)}), bf16[8,128,640]{2,1,0:T(8,128)(2,1)S(1)}, u32[]{:S(2)}, u32[]{:S(2)}) %all-to-all-start.1) | async-done | bytes 1310752 | tf_op jit(solution)/shard_map/all_to_all | solution.py:481
  188.1 0.7 broadcast_in_dim.17
  188.8 5.0 %all-to-all-start.6 = ((f32[32,3,2,128]{3,2,1,0:T(2,128)}), f32[32,3,2,128]{3,2,1,0:T(2,128)S(1)}, u32[]{:S(2)}, u32[]{:S(2)}) async-start(f32[32,3,2,128]{3,2,1,0:T(2,128)} %broadcast_in_dim.17), calls=%async_computation.6 | async-start | bytes 196608 | tf_op jit(solution)/shard_map/all_to_all | solution.py:37
  193.8 3.2 %shard_map.139 = bf16[128,1024]{1,0:T(8,128)(2,1)} custom-call(bf16[8,128,640]{2,1,0:T(8,128)(2,1)} %copy-done), custom_call_target="tpu_custom_call" | custom-call | tf_op jit(solution)/shard_map/pallas_call | solution.py:397
  197.0 4.1 %all-to-all-done.6 = f32[32,3,2,128]{3,2,1,0:T(2,128)S(1)} async-done(((f32[32,3,2,128]{3,2,1,0:T(2,128)}), f32[32,3,2,128]{3,2,1,0:T(2,128)S(1)}, u32[]{:S(2)}, u32[]{:S(2)}) %all-to-all-start.6) | async-done | bytes 98336 | tf_op jit(solution)/shard_map/all_to_all | solution.py:37
  (92 shorter events, 4.3 us)
Async XLA Ops:
  0.6 45.3 %copy-start.16 = (s32[8]{0:T(128)S(1)}, s32[8]{0:T(128)}, u32[]{:S(2)}) copy-start(s32[8]{0:T(128)} %param.15) | copy-start | bytes 100
  1.5 6.9 %collective-permute-start.3 = (bf16[128,256]{1,0:T(8,128)(2,1)S(1)}, bf16[128,256]{1,0:T(8,128)(2,1)S(1)}, u32[]{:S(2)}, u32[]{:S(2)}) collective-permute-start(bf16[128,256]{1,0:T(8,128)(2,1)S(1)} %pad_maximum_fusion.3), channel_id=1, source_target_pairs={{0,34},{2,32},{4,102},{6,100},{8,170},{10,168},{12,238},{14,236},{... | collective-permute-start | bytes 196616 | tf_op jit(solution)/shard_map/ppermute | solution.py:461
  5.9 2.5 %collective-permute-start.1 = (bf16[128,256]{1,0:T(8,128)(2,1)S(1)}, bf16[128,256]{1,0:T(8,128)(2,1)S(1)}, u32[]{:S(2)}, u32[]{:S(2)}) collective-permute-start(bf16[128,256]{1,0:T(8,128)(2,1)S(1)} %pad_maximum_fusion.3), channel_id=1, source_target_pairs={{0,2},{2,0},{4,70},{6,68},{8,138},{10,136},{12,206},{14,204},{16,1... | collective-permute-start | bytes 196616 | tf_op jit(solution)/shard_map/ppermute | solution.py:461
  5.9 4.7 %collective-permute-start.2 = (bf16[128,256]{1,0:T(8,128)(2,1)S(1)}, bf16[128,256]{1,0:T(8,128)(2,1)S(1)}, u32[]{:S(2)}, u32[]{:S(2)}) collective-permute-start(bf16[128,256]{1,0:T(8,128)(2,1)S(1)} %pad_maximum_fusion.2), channel_id=1, source_target_pairs={{0,32},{2,34},{4,100},{6,102},{8,168},{10,170},{12,236},{14,238},{... | collective-permute-start | bytes 196616 | tf_op jit(solution)/shard_map/ppermute | solution.py:461
  7.7 2.9 %collective-permute-start = (bf16[128,256]{1,0:T(8,128)(2,1)S(1)}, bf16[128,256]{1,0:T(8,128)(2,1)S(1)}, u32[]{:S(2)}, u32[]{:S(2)}) collective-permute-start(bf16[128,256]{1,0:T(8,128)(2,1)S(1)} %pad_maximum_fusion.2), channel_id=1, source_target_pairs={{0,0},{2,2},{4,68},{6,70},{8,136},{10,138},{12,204},{14,206},{16,1... | collective-permute-start | bytes 196616 | tf_op jit(solution)/shard_map/ppermute | solution.py:461
  10.6 50.9 %copy-start.2 = (bf16[4,128,256]{2,1,0:T(8,128)(2,1)}, bf16[4,128,256]{2,1,0:T(8,128)(2,1)S(1)}, u32[]{:S(2)}) copy-start(bf16[4,128,256]{2,1,0:T(8,128)(2,1)S(1)} %pad_maximum_fusion) | copy-start | bytes 786436
  10.7 13.3 %collective-permute-start.8 = (bf16[2,2,128,256]{3,2,1,0:T(8,128)(2,1)S(1)}, bf16[2,2,128,256]{3,2,1,0:T(8,128)(2,1)S(1)}, u32[]{:S(2)}, u32[]{:S(2)}) collective-permute-start(bf16[2,2,128,256]{3,2,1,0:T(8,128)(2,1)S(1)} %bitcast.70), channel_id=1, source_target_pairs={{0,28},{4,0},{8,4},{12,8},{16,12},{20,16},{24,20},{28,24},{1,29},{... | collective-permute-start | bytes 786440 | tf_op jit(solution)/shard_map/ppermute | solution.py:465
  19.9 8.3 %collective-permute-start.4 = (bf16[2,2,128,256]{3,2,1,0:T(8,128)(2,1)S(1)}, bf16[2,2,128,256]{3,2,1,0:T(8,128)(2,1)S(1)}, u32[]{:S(2)}, u32[]{:S(2)}) collective-permute-start(bf16[2,2,128,256]{3,2,1,0:T(8,128)(2,1)S(1)} %bitcast.71), channel_id=1, source_target_pairs={{0,4},{4,8},{8,12},{12,16},{16,20},{20,24},{24,28},{28,0},{1,5},{5... | collective-permute-start | bytes 786440 | tf_op jit(solution)/shard_map/ppermute | solution.py:465
  23.9 37.6 %copy-start.6 = (bf16[2,2,128,256]{3,2,1,0:T(8,128)(2,1)}, bf16[2,2,128,256]{3,2,1,0:T(8,128)(2,1)S(1)}, u32[]{:S(2)}) copy-start(bf16[2,2,128,256]{3,2,1,0:T(8,128)(2,1)S(1)} %collective-permute-done.8.refs_7_) | copy-start | bytes 786436
  23.9 6.8 %collective-permute-start.9 = (bf16[2,2,128,256]{3,2,1,0:T(8,128)(2,1)S(1)}, bf16[2,2,128,256]{3,2,1,0:T(8,128)(2,1)S(1)}, u32[]{:S(2)}, u32[]{:S(2)}) collective-permute-start(bf16[2,2,128,256]{3,2,1,0:T(8,128)(2,1)S(1)} %collective-permute-done.8.refs_7_), channel_id=1, source_target_pairs={{0,28},{4,0},{8,4},{12,8},{16,12},{20,16},{24,20},{28,24},{1,29},{... | collective-permute-start | bytes 786440 | tf_op jit(solution)/shard_map/ppermute | solution.py:465
  28.1 33.4 %copy-start.7 = (bf16[2,2,128,256]{3,2,1,0:T(8,128)(2,1)}, bf16[2,2,128,256]{3,2,1,0:T(8,128)(2,1)S(1)}, u32[]{:S(2)}) copy-start(bf16[2,2,128,256]{3,2,1,0:T(8,128)(2,1)S(1)} %collective-permute-done.4.refs_1_) | copy-start | bytes 786436
  28.1 17.7 %collective-permute-start.5 = (bf16[2,2,128,256]{3,2,1,0:T(8,128)(2,1)S(1)}, bf16[2,2,128,256]{3,2,1,0:T(8,128)(2,1)S(1)}, u32[]{:S(2)}, u32[]{:S(2)}) collective-permute-start(bf16[2,2,128,256]{3,2,1,0:T(8,128)(2,1)S(1)} %collective-permute-done.4.refs_1_), channel_id=1, source_target_pairs={{0,4},{4,8},{8,12},{12,16},{16,20},{20,24},{24,28},{28,0},{1,5},{5... | collective-permute-start | bytes 786440 | tf_op jit(solution)/shard_map/ppermute | solution.py:465
  30.7 30.8 %copy-start.8 = (bf16[2,2,128,256]{3,2,1,0:T(8,128)(2,1)}, bf16[2,2,128,256]{3,2,1,0:T(8,128)(2,1)S(1)}, u32[]{:S(2)}) copy-start(bf16[2,2,128,256]{3,2,1,0:T(8,128)(2,1)S(1)} %collective-permute-done.9.refs_6_) | copy-start | bytes 786436
  30.7 15.4 %collective-permute-start.10 = (bf16[2,2,128,256]{3,2,1,0:T(8,128)(2,1)S(1)}, bf16[2,2,128,256]{3,2,1,0:T(8,128)(2,1)S(1)}, u32[]{:S(2)}, u32[]{:S(2)}) collective-permute-start(bf16[2,2,128,256]{3,2,1,0:T(8,128)(2,1)S(1)} %collective-permute-done.9.refs_6_), channel_id=1, source_target_pairs={{0,28},{4,0},{8,4},{12,8},{16,12},{20,16},{24,20},{28,24},{1,29},{... | collective-permute-start | bytes 786440 | tf_op jit(solution)/shard_map/ppermute | solution.py:465
  36.0 25.6 %all-to-all-start = ((bf16[8,136,512]{2,1,0:T(8,128)(2,1)}), bf16[8,136,512]{2,1,0:T(8,128)(2,1)S(1)}, u32[]{:S(2)}, u32[]{:S(2)}) async-start(bf16[8,136,512]{2,1,0:T(8,128)(2,1)} %queries_to_send.1), calls=%async_computation | async-start | bytes 2228224 | tf_op jit(solution)/shard_map/all_to_all | solution.py:474
  45.9 15.7 %copy-start.9 = (bf16[2,2,128,256]{3,2,1,0:T(8,128)(2,1)}, bf16[2,2,128,256]{3,2,1,0:T(8,128)(2,1)S(1)}, u32[]{:S(2)}) copy-start(bf16[2,2,128,256]{3,2,1,0:T(8,128)(2,1)S(1)} %collective-permute-done.5.refs_2_) | copy-start | bytes 786436
  45.9 9.1 %collective-permute-start.6 = (bf16[2,2,128,256]{3,2,1,0:T(8,128)(2,1)S(1)}, bf16[2,2,128,256]{3,2,1,0:T(8,128)(2,1)S(1)}, u32[]{:S(2)}, u32[]{:S(2)}) collective-permute-start(bf16[2,2,128,256]{3,2,1,0:T(8,128)(2,1)S(1)} %collective-permute-done.5.refs_2_), channel_id=1, source_target_pairs={{0,4},{4,8},{8,12},{12,16},{16,20},{20,24},{24,28},{28,0},{1,5},{5... | collective-permute-start | bytes 786440 | tf_op jit(solution)/shard_map/ppermute | solution.py:465
  46.2 15.4 %copy-start.3 = (bf16[2,2,128,256]{3,2,1,0:T(8,128)(2,1)}, bf16[2,2,128,256]{3,2,1,0:T(8,128)(2,1)S(1)}, u32[]{:S(2)}) copy-start(bf16[2,2,128,256]{3,2,1,0:T(8,128)(2,1)S(1)} %collective-permute-done.10.refs_5_) | copy-start | bytes 786436
  46.2 9.6 %collective-permute-start.11 = (bf16[2,128,256]{2,1,0:T(8,128)(2,1)S(1)}, bf16[2,128,256]{2,1,0:T(8,128)(2,1)S(1)}, u32[]{:S(2)}, u32[]{:S(2)}) collective-permute-start(bf16[2,128,256]{2,1,0:T(8,128)(2,1)S(1)} %slice_bitcast_fusion), channel_id=1, source_target_pairs={{0,28},{4,0},{8,4},{12,8},{16,12},{20,16},{24,20},{28,24},{1,29},{... | collective-permute-start | bytes 393224 | tf_op jit(solution)/shard_map/ppermute | solution.py:465
  55.0 6.6 %copy-start.4 = (bf16[2,2,128,256]{3,2,1,0:T(8,128)(2,1)}, bf16[2,2,128,256]{3,2,1,0:T(8,128)(2,1)S(1)}, u32[]{:S(2)}) copy-start(bf16[2,2,128,256]{3,2,1,0:T(8,128)(2,1)S(1)} %collective-permute-done.6.refs_3_) | copy-start | bytes 786436
  55.0 5.5 %collective-permute-start.7 = (bf16[2,128,256]{2,1,0:T(8,128)(2,1)S(1)}, bf16[2,128,256]{2,1,0:T(8,128)(2,1)S(1)}, u32[]{:S(2)}, u32[]{:S(2)}) collective-permute-start(bf16[2,128,256]{2,1,0:T(8,128)(2,1)S(1)} %slice_bitcast_fusion.1), channel_id=1, source_target_pairs={{0,4},{4,8},{8,12},{12,16},{16,20},{20,24},{24,28},{28,0},{1,5},{5... | collective-permute-start | bytes 393224 | tf_op jit(solution)/shard_map/ppermute | solution.py:465
  61.6 1.0 copy-start.1
  69.9 10.7 %all-to-all-start.2 = ((bf16[8,8,640]{2,1,0:T(8,128)(2,1)}), bf16[8,8,640]{2,1,0:T(8,128)(2,1)S(1)}, u32[]{:S(2)}, u32[]{:S(2)}) async-start(bf16[8,8,640]{2,1,0:T(8,128)(2,1)} %chosen_attention.1), calls=%async_computation.2 | async-start | bytes 163840 | tf_op jit(solution)/shard_map/all_to_all | solution.py:476
  80.6 0.6 copy-start.5
  82.9 4.6 %copy-start.10 = (bf16[4,2048]{1,0:T(4,128)(2,1)S(1)}, bf16[4,2048]{1,0:T(4,128)(2,1)}, u32[]{:S(2)}) copy-start(bf16[4,2048]{1,0:T(4,128)(2,1)} %param.17) | copy-start | bytes 49156
  82.9 7.7 %copy-start.12 = (f32[2048]{0:T(1024)S(1)}, f32[2048]{0:T(1024)}, u32[]{:S(2)}) copy-start(f32[2048]{0:T(1024)} %param.18) | copy-start | bytes 24580
  82.9 12.4 %copy-start.13 = (s32[512]{0:T(512)S(1)}, s32[512]{0:T(512)}, u32[]{:S(2)}) copy-start(s32[512]{0:T(512)} %param.21) | copy-start | bytes 6148
  87.6 2.9 %collective-permute-start.12 = (bf16[4,4096]{1,0:T(4,128)(2,1)S(1)}, bf16[4,4096]{1,0:T(4,128)(2,1)S(1)}, u32[]{:S(2)}, u32[]{:S(2)}) collective-permute-start(bf16[4,4096]{1,0:T(4,128)(2,1)S(1)} %convert_element_type.25), channel_id=1, source_target_pairs={{0,1},{1,0},{2,3},{3,2},{4,5},{5,4},{6,7},{7,6},{8,9},{9,8},{10,11... | collective-permute-start | bytes 98312 | tf_op jit(solution)/shard_map/ppermute | solution.py:43
  91.5 13.0 %all-to-all-start.3 = ((bf16[16,4,2048]{2,1,0:T(4,128)(2,1)}), bf16[16,4,2048]{2,1,0:T(4,128)(2,1)S(1)}, u32[]{:S(2)}, u32[]{:S(2)}) async-start(bf16[16,4,2048]{2,1,0:T(4,128)(2,1)} %broadcast_in_dim.12), calls=%async_computation.3 | async-start | bytes 524288 | tf_op jit(solution)/shard_map/all_to_all | solution.py:37
  106.0 14.9 %all-to-all-start.4 = ((bf16[4,16,4,2048]{3,2,1,0:T(4,128)(2,1)}), bf16[4,16,4,2048]{3,2,1,0:T(4,128)(2,1)S(1)}, u32[]{:S(2)}, u32[]{:S(2)}) async-start(bf16[4,16,4,2048]{3,2,1,0:T(4,128)(2,1)} %broadcast_in_dim.14), calls=%async_computation.4 | async-start | bytes 2097152 | tf_op jit(solution)/shard_map/all_to_all | solution.py:37
  121.1 16.3 %collective-permute-start.14 = (bf16[256,2048]{1,0:T(8,128)(2,1)S(1)}, bf16[256,2048]{1,0:T(8,128)(2,1)}, u32[]{:S(2)}, u32[]{:S(2)}) collective-permute-start(bf16[256,2048]{1,0:T(8,128)(2,1)S(1)} %reshape.119), channel_id=1, source_target_pairs={{0,2},{2,0},{1,3},{3,1},{4,6},{6,4},{5,7},{7,5},{8,10},{10,8},{9,1... | collective-permute-start | bytes 3145736 | tf_op jit(solution)/shard_map/ppermute | solution.py:500
  129.4 7.8 %collective-permute-start.13 = (bf16[128,1002]{0,1:T(8,128)(2,1)S(1)}, bf16[128,1002]{0,1:T(8,128)(2,1)S(1)}, u32[]{:S(2)}, u32[]{:S(2)}) collective-permute-start(bf16[128,1002]{0,1:T(8,128)(2,1)S(1)} %dynamic-slice_convert_fusion.1), channel_id=1, source_target_pairs={{0,1},{1,0},{2,3},{3,2},{4,5},{5,4},{6,7},{7,6},{8,9},{9,8},{10,11... | collective-permute-start | bytes 769544 | tf_op jit(solution)/shard_map/ppermute | solution.py:43
  141.2 7.2 %collective-permute-start.15 = (bf16[128,1002]{0,1:T(8,128)(2,1)S(1)}, bf16[128,1002]{0,1:T(8,128)(2,1)S(1)}, u32[]{:S(2)}, u32[]{:S(2)}) collective-permute-start(bf16[128,1002]{0,1:T(8,128)(2,1)S(1)} %dynamic-slice_convert_fusion), channel_id=1, source_target_pairs={{0,1},{1,0},{2,3},{3,2},{4,5},{5,4},{6,7},{7,6},{8,9},{9,8},{10,11... | collective-permute-start | bytes 769544 | tf_op jit(solution)/shard_map/ppermute | solution.py:43
  149.4 15.7 %all-to-all-start.5 = ((f32[8,2,3,128]{3,1,2,0:T(2,128)}), f32[8,2,3,128]{3,1,2,0:T(2,128)S(1)}, u32[]{:S(2)}, u32[]{:S(2)}) async-start(f32[8,2,3,128]{3,1,2,0:T(2,128)} %broadcast_in_dim.16), calls=%async_computation.5 | async-start | bytes 49152 | tf_op jit(solution)/shard_map/all_to_all | solution.py:37
  165.1 36.4 %copy-start.14 = (f32[512]{0:T(512)S(1)}, f32[512]{0:T(512)}, u32[]{:S(2)}) copy-start(f32[512]{0:T(512)} %param.23) | copy-start | bytes 6148
  165.1 36.4 %copy-start.15 = (f32[512]{0:T(512)S(1)}, f32[512]{0:T(512)}, u32[]{:S(2)}) copy-start(f32[512]{0:T(512)} %param.22) | copy-start | bytes 6148
  165.1 22.9 %all-to-all-start.1 = ((bf16[8,128,640]{2,1,0:T(8,128)(2,1)}), bf16[8,128,640]{2,1,0:T(8,128)(2,1)S(1)}, u32[]{:S(2)}, u32[]{:S(2)}) async-start(bf16[8,128,640]{2,1,0:T(8,128)(2,1)} %partial_attention.7), calls=%async_computation.1 | async-start | bytes 2621440 | tf_op jit(solution)/shard_map/all_to_all | solution.py:481
  188.1 5.7 %copy-start = (bf16[8,128,640]{2,1,0:T(8,128)(2,1)}, bf16[8,128,640]{2,1,0:T(8,128)(2,1)S(1)}, u32[]{:S(2)}) copy-start(bf16[8,128,640]{2,1,0:T(8,128)(2,1)S(1)} %all-to-all-done.1.parts_ref) | copy-start | bytes 3932164
  188.8 12.4 %all-to-all-start.6 = ((f32[32,3,2,128]{3,2,1,0:T(2,128)}), f32[32,3,2,128]{3,2,1,0:T(2,128)S(1)}, u32[]{:S(2)}, u32[]{:S(2)}) async-start(f32[32,3,2,128]{3,2,1,0:T(2,128)} %broadcast_in_dim.17), calls=%async_computation.6 | async-start | bytes 196608 | tf_op jit(solution)/shard_map/all_to_all | solution.py:37
  201.6 0.6 copy-start.11

commit v2 on v1

--- a/solution.py
+++ b/solution.py
@@ -175,7 +175,7 @@
         m_ref[...] = top
         return carry
 
-    lax.fori_loop(0, chunks, score_step, 0)
+    lax.fori_loop(0, chunks, score_step, 0, unroll=True)
     top = jnp.max(m_ref[...], axis=1, keepdims=True) * SCORE_TO_LOG2
     top = jnp.maximum(top, NO_TOP).astype(jnp.bfloat16).astype(jnp.float32)
     top = jnp.broadcast_to(top, m_ref.shape)
@@ -190,7 +190,7 @@
         )
         return carry
 
-    lax.fori_loop(0, chunks, weigh_step, 0)
+    lax.fori_loop(0, chunks, weigh_step, 0, unroll=True)
     tops, totals = [], []
     for g in range(GROUP):
         at = slice(g * each, (g + 1) * each)
@@ -364,7 +364,7 @@
     )(meta, q_all, *kv_all, before)
 
 
-def merge_kernel(parts_ref, merged_ref):
+def merge_parts(parts_ref, merged_ref):
     windows = parts_ref.shape[0] // 2
     rows = parts_ref.shape[1]
     for c in range(2):
@@ -392,6 +392,39 @@
             merged_ref[:, at : at + HEAD_SIZE] = result.astype(jnp.bfloat16)
 
 
+def merge_kernel(parts_ref, merged_ref):
+    merge_parts(parts_ref, merged_ref)
+
+
+def project_kernel(parts_ref, weight_ref, out_ref, chosen_ref):
+    @pl.when(pl.program_id(0) == 0)
+    def _():
+        merge_parts(parts_ref, chosen_ref)
+
+    out_ref[...] = jnp.dot(
+        chosen_ref[...], weight_ref[...], preferred_element_type=jnp.float32
+    )
+
+
+def projected_rows(parts, out_weight):
+    rows = parts.shape[1]
+    features, width = out_weight.shape
+    block = width // 8
+    return pl.pallas_call(
+        project_kernel,
+        grid=(width // block,),
+        in_specs=[
+            pl.BlockSpec(parts.shape, lambda n: (0, 0, 0)),
+            pl.BlockSpec((features, block), lambda n: (0, n)),
+        ],
+        out_specs=pl.BlockSpec((rows, block), lambda n: (0, n)),
+        out_shape=jax.ShapeDtypeStruct((rows, width), jnp.float32),
+        scratch_shapes=[pltpu.VMEM((rows, features), jnp.bfloat16)],
+        compiler_params=pltpu.CompilerParams(dimension_semantics=("arbitrary",)),
+        name="projected_rows",
+    )(parts, out_weight)
+
+
 def merged_attention(parts):
     rows = parts.shape[1]
     return pl.pallas_call(
@@ -399,6 +432,7 @@
         in_specs=[pl.BlockSpec(memory_space=pltpu.VMEM)],
         out_specs=pl.BlockSpec(memory_space=pltpu.VMEM),
         out_shape=jax.ShapeDtypeStruct((rows, 2 * GROUP * HEAD_SIZE), jnp.bfloat16),
+        name="merged_attention",
     )(parts)
 
 
@@ -474,16 +508,15 @@
     q_all = lax.all_to_all(q_send, XC, 0, 0, tiled=True)
     few = chosen_attention(meta, q_all, kv_all)
     few = lax.all_to_all(few, XC, 0, 0, tiled=True)
-    chosen = merged_attention(few)
+    partial_value = projected_rows(few, out_weight)[:count]
     parts = q_all
-    for n in range(nx):
-        parts = partial_attention(meta, q_all, kv_all, n, 1, parts)
+    for first, number in ((0, 1), (1, 1), (2, nx - 2)):
+        parts = partial_attention(meta, q_all, kv_all, first, number, parts)
     arrived = lax.all_to_all(parts, XC, 0, 0, tiled=True)
     attended = merged_attention(arrived)
 
     half = residual.shape[1]
     head = lax.axis_index("head")
-    partial_value = jnp.dot(chosen, out_weight, preferred_element_type=jnp.float32)[:count]
     own = lax.dynamic_slice_in_dim(partial_value, head * half, half, 1)
     own = own + residual.astype(jnp.float32)
     partial_value = lax.dynamic_update_slice_in_dim(partial_value, own, head * half, 1)
@@ -506,10 +539,13 @@
     ids = lax.dynamic_index_in_dim(ids, head, 1, keepdims=False) - my_index * vocab_rows
 
     def local_stats(normed_rows, local_ids):
-        partial_logits = jnp.dot(normed_rows, lm_weight, preferred_element_type=jnp.float32)
+        partial_logits = jnp.dot(
+            normed_rows, lm_weight, preferred_element_type=jnp.float32
+        )
         theirs = lax.dynamic_slice_in_dim(partial_logits, (1 - head) * rows, rows, 0)
         ours = lax.dynamic_slice_in_dim(partial_logits, head * rows, rows, 0)
-        logits = ours + swap_heads(theirs.astype(jnp.bfloat16)).astype(jnp.float32)
+        theirs = swap_heads(theirs.astype(jnp.bfloat16))
+        logits = ours + theirs.astype(jnp.float32)
         matches = local_ids[:, None] == jnp.arange(vocab_rows, dtype=jnp.int32)[None, :]
         target_part = jnp.sum(jnp.where(matches, logits, 0.0), axis=1)
         local_top = jnp.max(logits, axis=1)

time: 203 us -> 206 us (1.015)
  blocking collectives: 0 us -> 12 us
  starting transfers between devices: 71.4 us -> 64.5 us
  matrix products: 11.9 us -> 7.25 us
    all_to_all x0 -> x1, blocking collectives: none -> 12 us  [spread(): lax.all_to_all(jnp.broadcast_to(shard[None], (n, *shard.shape)), axes, 0,...]
    pallas_call x0 -> x1, Pallas kernels: none -> 7.55 us  [projected_rows(): pl.pallas_call(project_kernel, grid=(width // block,), in_specs=[pl.Block...]
    all_to_all x4 -> x3, starting transfers between devices: 18.4 us -> 11.8 us  [spread(): lax.all_to_all(jnp.broadcast_to(shard[None], (n, *shard.shape)), axes, 0,...]
    dot_general x1 -> x0, matrix products: 4.63 us -> none  [per_device(): jnp.dot(chosen, out_weight, preferred_element_type=jnp.float32)[:count]]
    pallas_call x4 -> x3, Pallas kernels: 28 us -> 24.6 us  [partial_attention(): pl.pallas_call(functools.partial(attention_kernel, first), grid_spec=pltp...]
    all_to_all x4 -> x3, waiting for transfers between devices: 13.6 us -> 10.4 us  [spread(): lax.all_to_all(jnp.broadcast_to(shard[None], (n, *shard.shape)), axes, 0,...]
    ppermute x3, waiting for transfers between devices: 8.11 us -> 10.6 us  [swap_heads(): return lax.ppermute(shard, 'head', [(0, 1), (1, 0)])]
    pallas_call x2 -> x1, Pallas kernels: 4.88 us -> 3.19 us  [merged_attention(): pl.pallas_call(merge_kernel, in_specs=[pl.BlockSpec(memory_space=pltpu.VM...]
  transfers between devices with their start and end apart: 23 -> 22, of which waited for: 15 -> 14; matrix products, arithmetic and copies ran while one was open for 3% -> 3% of each run, Pallas kernels for 16% -> 15%
where the time goes in v2:
time: 206 us; the launch traced here: 203 us
  starting transfers between devices  64.5 us (31%)
  waiting for transfers between devices  64.3 us (31%)
  Pallas kernels  43.7 us (21%)
  blocking collectives  12 us (6%)
  local copies, waits for them, and re-layouts  7.9 us (4%)
  matrix products  7.25 us (4%)
  other arithmetic  2.76 us (1%)
    pallas_call x3, Pallas kernels, partial_attention(): pl.pallas_call(functools.partial(attention_kernel, first), grid_spec=pltp...  24.6 us
    ppermute x8, starting transfers between devices, shifted(): return lax.ppermute(a, 'ctx_2', [(k, (k + d) % nz) for k in range(nz)])  18.7 us
    ppermute x8, waiting for transfers between devices, shifted(): return lax.ppermute(a, 'ctx_2', [(k, (k + d) % nz) for k in range(nz)])  18.2 us
    all_to_all x1, waiting for transfers between devices, per_device(): arrived = lax.all_to_all(parts, XC, 0, 0, tiled=True)  17.7 us
    all_to_all x1, blocking collectives, spread(): lax.all_to_all(jnp.broadcast_to(shard[None], (n, *shard.shape)), axes, 0,...  12 us
    all_to_all x3, starting transfers between devices, spread(): lax.all_to_all(jnp.broadcast_to(shard[None], (n, *shard.shape)), axes, 0,...  11.8 us
    ppermute x3, waiting for transfers between devices, swap_heads(): return lax.ppermute(shard, 'head', [(0, 1), (1, 0)])  10.6 us
    all_to_all x3, waiting for transfers between devices, spread(): lax.all_to_all(jnp.broadcast_to(shard[None], (n, *shard.shape)), axes, 0,...  10.4 us
  transfers between devices with their start and end apart: 22, of which 14 were waited for; matrix products, arithmetic and copies ran while one was open for 3% of the time, Pallas kernels for 15%

profile of v2, /device:TPU:1, one launch (start us, length us, event | category | flops | bytes accessed | tf_op | source)
XLA Modules:
  0.0 203.4 jit_solution(2206797419593038808)
XLA Ops:
  0.6 0.8 constant_dynamic-slice_fusion.5
  1.5 4.4 %collective-permute-start.3 = (bf16[128,256]{1,0:T(8,128)(2,1)S(1)}, bf16[128,256]{1,0:T(8,128)(2,1)S(1)}, u32[]{:S(2)}, u32[]{:S(2)}) collective-permute-start(bf16[128,256]{1,0:T(8,128)(2,1)S(1)} %pad_maximum_fusion.3), channel_id=1, source_target_pairs={{0,34},{2,32},{4,102},{6,100},{8,170},{10,168},{12,238},{14,236},{... | collective-permute-start | bytes 196616 | tf_op jit(solution)/shard_map/ppermute | solution.py:495
  5.9 1.9 collective-permute-start.2
  7.7 0.7 collective-permute-start
  8.4 2.2 %collective-permute-done.2 = bf16[128,256]{1,0:T(8,128)(2,1)S(1)} collective-permute-done((bf16[128,256]{1,0:T(8,128)(2,1)S(1)}, bf16[128,256]{1,0:T(8,128)(2,1)S(1)}, u32[]{:S(2)}, u32[]{:S(2)}) %collective-permute-start.2) | collective-permute-done | bytes 65568 | tf_op jit(solution)/shard_map/ppermute | solution.py:495
  10.7 9.2 %collective-permute-start.8 = (bf16[2,2,128,256]{3,2,1,0:T(8,128)(2,1)S(1)}, bf16[2,2,128,256]{3,2,1,0:T(8,128)(2,1)S(1)}, u32[]{:S(2)}, u32[]{:S(2)}) collective-permute-start(bf16[2,2,128,256]{3,2,1,0:T(8,128)(2,1)S(1)} %bitcast.69), channel_id=1, source_target_pairs={{0,28},{4,0},{8,4},{12,8},{16,12},{20,16},{24,20},{28,24},{1,29},{... | collective-permute-start | bytes 786440 | tf_op jit(solution)/shard_map/ppermute | solution.py:499
  19.9 4.1 %collective-permute-done.8.refs_7_ = bf16[2,2,128,256]{3,2,1,0:T(8,128)(2,1)S(1)} collective-permute-done((bf16[2,2,128,256]{3,2,1,0:T(8,128)(2,1)S(1)}, bf16[2,2,128,256]{3,2,1,0:T(8,128)(2,1)S(1)}, u32[]{:S(2)}, u32[]{:S(2)}) %collective-permute-start.8) | collective-permute-done | bytes 262176 | tf_op jit(solution)/shard_map/ppermute | solution.py:499
  23.9 3.5 %collective-permute-start.9 = (bf16[2,2,128,256]{3,2,1,0:T(8,128)(2,1)S(1)}, bf16[2,2,128,256]{3,2,1,0:T(8,128)(2,1)S(1)}, u32[]{:S(2)}, u32[]{:S(2)}) collective-permute-start(bf16[2,2,128,256]{3,2,1,0:T(8,128)(2,1)S(1)} %collective-permute-done.8.refs_7_), channel_id=1, source_target_pairs={{0,28},{4,0},{8,4},{12,8},{16,12},{20,16},{24,20},{28,24},{1,29},{... | collective-permute-start | bytes 786440 | tf_op jit(solution)/shard_map/ppermute | solution.py:499
  27.4 0.7 collective-permute-done.4.refs_1_
  28.1 2.6 %collective-permute-done.9.refs_6_ = bf16[2,2,128,256]{3,2,1,0:T(8,128)(2,1)S(1)} collective-permute-done((bf16[2,2,128,256]{3,2,1,0:T(8,128)(2,1)S(1)}, bf16[2,2,128,256]{3,2,1,0:T(8,128)(2,1)S(1)}, u32[]{:S(2)}, u32[]{:S(2)}) %collective-permute-start.9) | collective-permute-done | bytes 262176 | tf_op jit(solution)/shard_map/ppermute | solution.py:499
  30.7 3.1 %collective-permute-start.10 = (bf16[2,2,128,256]{3,2,1,0:T(8,128)(2,1)S(1)}, bf16[2,2,128,256]{3,2,1,0:T(8,128)(2,1)S(1)}, u32[]{:S(2)}, u32[]{:S(2)}) collective-permute-start(bf16[2,2,128,256]{3,2,1,0:T(8,128)(2,1)S(1)} %collective-permute-done.9.refs_6_), channel_id=1, source_target_pairs={{0,28},{4,0},{8,4},{12,8},{16,12},{20,16},{24,20},{28,24},{1,29},{... | collective-permute-start | bytes 786440 | tf_op jit(solution)/shard_map/ppermute | solution.py:499
  33.8 2.1 %queries_to_send.1 = bf16[8,136,512]{2,1,0:T(8,128)(2,1)} custom-call(s32[4]{0:T(128)} %scored_ref.1, bf16[128,1024]{1,0:T(8,128)(2,1)} %q_ref.1), custom_call_target="tpu_custom_call" | custom-call | tf_op jit(solution)/shard_map/queries_to_send/pallas_call | solution.py:114
  36.0 9.9 %all-to-all-start = ((bf16[8,136,512]{2,1,0:T(8,128)(2,1)}), bf16[8,136,512]{2,1,0:T(8,128)(2,1)S(1)}, u32[]{:S(2)}, u32[]{:S(2)}) async-start(bf16[8,136,512]{2,1,0:T(8,128)(2,1)} %queries_to_send.1), calls=%async_computation | async-start | bytes 2228224 | tf_op jit(solution)/shard_map/all_to_all | solution.py:508
  46.2 2.7 %collective-permute-start.11 = (bf16[2,128,256]{2,1,0:T(8,128)(2,1)S(1)}, bf16[2,128,256]{2,1,0:T(8,128)(2,1)S(1)}, u32[]{:S(2)}, u32[]{:S(2)}) collective-permute-start(bf16[2,128,256]{2,1,0:T(8,128)(2,1)S(1)} %slice_bitcast_fusion), channel_id=1, source_target_pairs={{0,28},{4,0},{8,4},{12,8},{16,12},{20,16},{24,20},{28,24},{1,29},{... | collective-permute-start | bytes 393224 | tf_op jit(solution)/shard_map/ppermute | solution.py:499
  48.9 6.1 %collective-permute-done.6.refs_3_ = bf16[2,2,128,256]{3,2,1,0:T(8,128)(2,1)S(1)} collective-permute-done((bf16[2,2,128,256]{3,2,1,0:T(8,128)(2,1)S(1)}, bf16[2,2,128,256]{3,2,1,0:T(8,128)(2,1)S(1)}, u32[]{:S(2)}, u32[]{:S(2)}) %collective-permute-start.6) | collective-permute-done | bytes 262176 | tf_op jit(solution)/shard_map/ppermute | solution.py:499
  55.1 0.6 concatenate.17.meta_ref
  55.7 4.7 %collective-permute-done.7 = bf16[2,128,256]{2,1,0:T(8,128)(2,1)S(1)} collective-permute-done((bf16[2,128,256]{2,1,0:T(8,128)(2,1)S(1)}, bf16[2,128,256]{2,1,0:T(8,128)(2,1)S(1)}, u32[]{:S(2)}, u32[]{:S(2)}) %collective-permute-start.7) | collective-permute-done | bytes 131104 | tf_op jit(solution)/shard_map/ppermute | solution.py:499
  60.5 0.7 pad_maximum_fusion.1.refs_4_
  61.6 1.0 copy-done.1
  62.6 6.2 %chosen_attention.1 = bf16[8,8,640]{2,1,0:T(8,128)(2,1)} custom-call(s32[12]{0:T(128)} %concatenate.17.meta_ref, bf16[8,136,512]{2,1,0:T(8,128)(2,1)} %copy-done.1, bf16[2,2,128,256]{3,2,1,0:T(8,128)(2,1)} %bitcast.71, bf16[2,2,128,256]{3,2,1,0:T(8,128)(2,1)} %copy-done.7, bf16[2,2,128,256]{3,2,1,0:T(8,128)(2,1)} %copy-done.9, ...), custom_call_target="tpu_custom_call" | custom-call | tf_op jit(solution)/shard_map/chosen_attention/pallas_call | solution.py:212
  68.8 5.8 %all-to-all-start.2 = ((bf16[8,8,640]{2,1,0:T(8,128)(2,1)}), bf16[8,8,640]{2,1,0:T(8,128)(2,1)S(1)}, u32[]{:S(2)}, u32[]{:S(2)}) async-start(bf16[8,8,640]{2,1,0:T(8,128)(2,1)} %chosen_attention.1), calls=%async_computation.2 | async-start | bytes 163840 | tf_op jit(solution)/shard_map/all_to_all | solution.py:510
  74.6 4.9 %all-to-all-done.2.parts_ref = bf16[8,8,640]{2,1,0:T(8,128)(2,1)S(1)} async-done(((bf16[8,8,640]{2,1,0:T(8,128)(2,1)}), bf16[8,8,640]{2,1,0:T(8,128)(2,1)S(1)}, u32[]{:S(2)}, u32[]{:S(2)}) %all-to-all-start.2) | async-done | bytes 81952 | tf_op jit(solution)/shard_map/all_to_all | solution.py:510
  79.5 0.6 copy-done.5
  80.1 7.6 %projected_rows.1 = f32[8,4096]{1,0:T(8,128)} custom-call(bf16[8,8,640]{2,1,0:T(8,128)(2,1)} %copy-done.5, bf16[1024,4096]{1,0:T(8,128)(2,1)} %weight_ref.1), custom_call_target="tpu_custom_call" | custom-call | tf_op jit(solution)/shard_map/projected_rows/pallas_call | solution.py:413
  87.7 0.9 slice.38
  88.8 2.8 %collective-permute-done.12 = bf16[4,4096]{1,0:T(4,128)(2,1)S(1)} collective-permute-done((bf16[4,4096]{1,0:T(4,128)(2,1)S(1)}, bf16[4,4096]{1,0:T(4,128)(2,1)S(1)}, u32[]{:S(2)}, u32[]{:S(2)}) %collective-permute-start.12) | collective-permute-done | bytes 32800 | tf_op jit(solution)/shard_map/ppermute | solution.py:43
  91.9 12.0 %all_to_all.35 = bf16[16,4,2048]{2,1,0:T(4,128)(2,1)S(1)} all-to-all(bf16[16,4,2048]{2,1,0:T(4,128)(2,1)S(1)} %broadcast_in_dim.12), channel_id=1, replica_groups=mesh['ctx_0'=4,'ctx_1'=2,'ctx_2'=8,'ctx_3'=2,'head'=2] {'ctx_1','ctx_2'}, dimensions={0} | all-to-all | bytes 524288 | tf_op jit(solution)/shard_map/all_to_all | solution.py:37
  103.9 1.5 broadcast_in_dim.14
  105.4 3.5 %all-to-all-start.4 = ((bf16[4,16,4,2048]{3,2,1,0:T(4,128)(2,1)}), bf16[4,16,4,2048]{3,2,1,0:T(4,128)(2,1)S(1)}, u32[]{:S(2)}, u32[]{:S(2)}) async-start(bf16[4,16,4,2048]{3,2,1,0:T(4,128)(2,1)} %broadcast_in_dim.14), calls=%async_computation.4 | async-start | bytes 2097152 | tf_op jit(solution)/shard_map/all_to_all | solution.py:37
  109.2 4.9 %partial_attention.3.refs_8_ = bf16[8,128,640]{2,1,0:T(8,128)(2,1)} custom-call(s32[12]{0:T(128)} %concatenate.17.meta_ref, bf16[8,136,512]{2,1,0:T(8,128)(2,1)} %copy-done.1, bf16[2,2,128,256]{3,2,1,0:T(8,128)(2,1)} %bitcast.72, bf16[2,2,128,256]{3,2,1,0:T(8,128)(2,1)} %copy-done.7, bf16[2,2,128,256]{3,2,1,0:T(8,128)(2,1)} %copy-done.9, ...), custom_call_target="tpu_custom_call" | custom-call | flops 5000000000 | bytes 4000000 | tf_op jit(solution)/shard_map/partial_attention/pallas_call | solution.py:339
  114.2 6.1 %all-to-all-done.4 = bf16[4,16,4,2048]{3,2,1,0:T(4,128)(2,1)S(1)} async-done(((bf16[4,16,4,2048]{3,2,1,0:T(4,128)(2,1)}), bf16[4,16,4,2048]{3,2,1,0:T(4,128)(2,1)S(1)}, u32[]{:S(2)}, u32[]{:S(2)}) %all-to-all-start.4) | async-done | bytes 1048608 | tf_op jit(solution)/shard_map/all_to_all | solution.py:37
  120.6 4.7 %collective-permute-start.14 = (bf16[256,2048]{1,0:T(8,128)(2,1)S(1)}, bf16[256,2048]{1,0:T(8,128)(2,1)}, u32[]{:S(2)}, u32[]{:S(2)}) collective-permute-start(bf16[256,2048]{1,0:T(8,128)(2,1)S(1)} %reshape.119), channel_id=1, source_target_pairs={{0,2},{2,0},{1,3},{3,1},{4,6},{6,4},{5,7},{7,5},{8,10},{10,8},{9,1... | collective-permute-start | bytes 3145736 | tf_op jit(solution)/shard_map/ppermute | solution.py:533
  125.3 3.5 %fusion.13 = f32[256,1002]{0,1:T(8,128)S(1)} fusion(bf16[256,2048]{1,0:T(8,128)(2,1)S(1)} %reshape.119, bf16[2048,1002]{0,1:T(8,128)(2,1)} %param.20), kind=kOutput, calls=%fused_computation.56 | convolution fusion | flops 1050673152 | bytes 6178816 | tf_op jit(solution)/shard_map/dot_general | solution.py:542
  129.3 5.9 %partial_attention.4.refs_8_ = bf16[8,128,640]{2,1,0:T(8,128)(2,1)} custom-call(s32[12]{0:T(128)} %concatenate.17.meta_ref, bf16[8,136,512]{2,1,0:T(8,128)(2,1)} %copy-done.1, bf16[2,2,128,256]{3,2,1,0:T(8,128)(2,1)} %bitcast.73, bf16[2,2,128,256]{3,2,1,0:T(8,128)(2,1)} %copy-done.7, ...), custom_call_target="tpu_custom_call", output_to_operand_aliasing={{}: (10, {})} | custom-call | flops 5000000000 | bytes 4000000 | tf_op jit(solution)/shard_map/partial_attention/pallas_call | solution.py:339
  135.1 1.5 collective-permute-done.13
  136.8 3.8 %fusion.14 = f32[256,1002]{0,1:T(8,128)S(1)} fusion(bf16[256,2048]{1,0:T(8,128)(2,1)} %collective-permute-done.14, bf16[2048,1002]{0,1:T(8,128)(2,1)} %param.20), kind=kOutput, calls=%fused_computation.57 | convolution fusion | flops 1050673152 | bytes 6178816 | tf_op jit(solution)/shard_map/dot_general | solution.py:542
  140.6 0.5 collective-permute-start.15
  141.3 6.3 %collective-permute-done.15 = bf16[128,1002]{0,1:T(8,128)(2,1)S(1)} collective-permute-done((bf16[128,1002]{0,1:T(8,128)(2,1)S(1)}, bf16[128,1002]{0,1:T(8,128)(2,1)S(1)}, u32[]{:S(2)}, u32[]{:S(2)}) %collective-permute-start.15) | collective-permute-done | bytes 256544 | tf_op jit(solution)/shard_map/ppermute | solution.py:43
  148.0 0.6 broadcast_in_dim.16
  148.6 3.8 %all-to-all-start.5 = ((f32[8,2,3,128]{3,1,2,0:T(2,128)}), f32[8,2,3,128]{3,1,2,0:T(2,128)S(1)}, u32[]{:S(2)}, u32[]{:S(2)}) async-start(f32[8,2,3,128]{3,1,2,0:T(2,128)} %broadcast_in_dim.16), calls=%async_computation.5 | async-start | bytes 49152 | tf_op jit(solution)/shard_map/all_to_all | solution.py:37
  152.4 13.8 %partial_attention.5 = bf16[8,128,640]{2,1,0:T(8,128)(2,1)} custom-call(s32[12]{0:T(128)} %concatenate.17.meta_ref, bf16[8,136,512]{2,1,0:T(8,128)(2,1)} %copy-done.1, bf16[2,2,128,256]{3,2,1,0:T(8,128)(2,1)} %bitcast.74, bf16[2,2,128,256]{3,2,1,0:T(8,128)(2,1)} %copy-done.7, bf16[2,2,128,256]{3,2,1,0:T(8,128)(2,1)} %copy-done.9, ...), custom_call_target="tpu_custom_call", output_to_operand_aliasing={{}: (10, {})} | custom-call | flops 10000000000 | bytes 4000000 | tf_op jit(solution)/shard_map/partial_attention/pallas_call | solution.py:339
  166.3 5.6 %all-to-all-start.1 = ((bf16[8,128,640]{2,1,0:T(8,128)(2,1)}), bf16[8,128,640]{2,1,0:T(8,128)(2,1)S(1)}, u32[]{:S(2)}, u32[]{:S(2)}) async-start(bf16[8,128,640]{2,1,0:T(8,128)(2,1)} %partial_attention.5), calls=%async_computation.1 | async-start | bytes 2621440 | tf_op jit(solution)/shard_map/all_to_all | solution.py:515
  172.0 17.7 %all-to-all-done.1.parts_ref = bf16[8,128,640]{2,1,0:T(8,128)(2,1)S(1)} async-done(((bf16[8,128,640]{2,1,0:T(8,128)(2,1)}), bf16[8,128,640]{2,1,0:T(8,128)(2,1)S(1)}, u32[]{:S(2)}, u32[]{:S(2)}) %all-to-all-start.1) | async-done | bytes 1310752 | tf_op jit(solution)/shard_map/all_to_all | solution.py:515
  189.7 0.7 broadcast_in_dim.17
  190.4 4.5 %all-to-all-start.6 = ((f32[32,3,2,128]{3,2,1,0:T(2,128)}), f32[32,3,2,128]{3,2,1,0:T(2,128)S(1)}, u32[]{:S(2)}, u32[]{:S(2)}) async-start(f32[32,3,2,128]{3,2,1,0:T(2,128)} %broadcast_in_dim.17), calls=%async_computation.6 | async-start | bytes 196608 | tf_op jit(solution)/shard_map/all_to_all | solution.py:37
  194.9 3.2 %merged_attention.1 = bf16[128,1024]{1,0:T(8,128)(2,1)} custom-call(bf16[8,128,640]{2,1,0:T(8,128)(2,1)} %copy-done), custom_call_target="tpu_custom_call" | custom-call | tf_op jit(solution)/shard_map/merged_attention/pallas_call | solution.py:430
  198.1 4.2 %all-to-all-done.6 = f32[32,3,2,128]{3,2,1,0:T(2,128)S(1)} async-done(((f32[32,3,2,128]{3,2,1,0:T(2,128)}), f32[32,3,2,128]{3,2,1,0:T(2,128)S(1)}, u32[]{:S(2)}, u32[]{:S(2)}) %all-to-all-start.6) | async-done | bytes 98336 | tf_op jit(solution)/shard_map/all_to_all | solution.py:37
  202.8 0.6 minimum_negate_fusion
  (90 shorter events, 3.6 us)
Async XLA Ops:
  0.6 45.3 %copy-start.16 = (s32[8]{0:T(128)S(1)}, s32[8]{0:T(128)}, u32[]{:S(2)}) copy-start(s32[8]{0:T(128)} %param.15) | copy-start | bytes 100
  1.5 6.9 %collective-permute-start.3 = (bf16[128,256]{1,0:T(8,128)(2,1)S(1)}, bf16[128,256]{1,0:T(8,128)(2,1)S(1)}, u32[]{:S(2)}, u32[]{:S(2)}) collective-permute-start(bf16[128,256]{1,0:T(8,128)(2,1)S(1)} %pad_maximum_fusion.3), channel_id=1, source_target_pairs={{0,34},{2,32},{4,102},{6,100},{8,170},{10,168},{12,238},{14,236},{... | collective-permute-start | bytes 196616 | tf_op jit(solution)/shard_map/ppermute | solution.py:495
  5.9 2.5 %collective-permute-start.1 = (bf16[128,256]{1,0:T(8,128)(2,1)S(1)}, bf16[128,256]{1,0:T(8,128)(2,1)S(1)}, u32[]{:S(2)}, u32[]{:S(2)}) collective-permute-start(bf16[128,256]{1,0:T(8,128)(2,1)S(1)} %pad_maximum_fusion.3), channel_id=1, source_target_pairs={{0,2},{2,0},{4,70},{6,68},{8,138},{10,136},{12,206},{14,204},{16,1... | collective-permute-start | bytes 196616 | tf_op jit(solution)/shard_map/ppermute | solution.py:495
  5.9 4.7 %collective-permute-start.2 = (bf16[128,256]{1,0:T(8,128)(2,1)S(1)}, bf16[128,256]{1,0:T(8,128)(2,1)S(1)}, u32[]{:S(2)}, u32[]{:S(2)}) collective-permute-start(bf16[128,256]{1,0:T(8,128)(2,1)S(1)} %pad_maximum_fusion.2), channel_id=1, source_target_pairs={{0,32},{2,34},{4,100},{6,102},{8,168},{10,170},{12,236},{14,238},{... | collective-permute-start | bytes 196616 | tf_op jit(solution)/shard_map/ppermute | solution.py:495
  7.7 2.9 %collective-permute-start = (bf16[128,256]{1,0:T(8,128)(2,1)S(1)}, bf16[128,256]{1,0:T(8,128)(2,1)S(1)}, u32[]{:S(2)}, u32[]{:S(2)}) collective-permute-start(bf16[128,256]{1,0:T(8,128)(2,1)S(1)} %pad_maximum_fusion.2), channel_id=1, source_target_pairs={{0,0},{2,2},{4,68},{6,70},{8,136},{10,138},{12,204},{14,206},{16,1... | collective-permute-start | bytes 196616 | tf_op jit(solution)/shard_map/ppermute | solution.py:495
  10.6 50.9 %copy-start.2 = (bf16[4,128,256]{2,1,0:T(8,128)(2,1)}, bf16[4,128,256]{2,1,0:T(8,128)(2,1)S(1)}, u32[]{:S(2)}) copy-start(bf16[4,128,256]{2,1,0:T(8,128)(2,1)S(1)} %pad_maximum_fusion) | copy-start | bytes 786436
  10.7 13.3 %collective-permute-start.8 = (bf16[2,2,128,256]{3,2,1,0:T(8,128)(2,1)S(1)}, bf16[2,2,128,256]{3,2,1,0:T(8,128)(2,1)S(1)}, u32[]{:S(2)}, u32[]{:S(2)}) collective-permute-start(bf16[2,2,128,256]{3,2,1,0:T(8,128)(2,1)S(1)} %bitcast.69), channel_id=1, source_target_pairs={{0,28},{4,0},{8,4},{12,8},{16,12},{20,16},{24,20},{28,24},{1,29},{... | collective-permute-start | bytes 786440 | tf_op jit(solution)/shard_map/ppermute | solution.py:499
  19.9 8.3 %collective-permute-start.4 = (bf16[2,2,128,256]{3,2,1,0:T(8,128)(2,1)S(1)}, bf16[2,2,128,256]{3,2,1,0:T(8,128)(2,1)S(1)}, u32[]{:S(2)}, u32[]{:S(2)}) collective-permute-start(bf16[2,2,128,256]{3,2,1,0:T(8,128)(2,1)S(1)} %bitcast.70), channel_id=1, source_target_pairs={{0,4},{4,8},{8,12},{12,16},{16,20},{20,24},{24,28},{28,0},{1,5},{5... | collective-permute-start | bytes 786440 | tf_op jit(solution)/shard_map/ppermute | solution.py:499
  23.9 37.6 %copy-start.6 = (bf16[2,2,128,256]{3,2,1,0:T(8,128)(2,1)}, bf16[2,2,128,256]{3,2,1,0:T(8,128)(2,1)S(1)}, u32[]{:S(2)}) copy-start(bf16[2,2,128,256]{3,2,1,0:T(8,128)(2,1)S(1)} %collective-permute-done.8.refs_7_) | copy-start | bytes 786436
  23.9 6.8 %collective-permute-start.9 = (bf16[2,2,128,256]{3,2,1,0:T(8,128)(2,1)S(1)}, bf16[2,2,128,256]{3,2,1,0:T(8,128)(2,1)S(1)}, u32[]{:S(2)}, u32[]{:S(2)}) collective-permute-start(bf16[2,2,128,256]{3,2,1,0:T(8,128)(2,1)S(1)} %collective-permute-done.8.refs_7_), channel_id=1, source_target_pairs={{0,28},{4,0},{8,4},{12,8},{16,12},{20,16},{24,20},{28,24},{1,29},{... | collective-permute-start | bytes 786440 | tf_op jit(solution)/shard_map/ppermute | solution.py:499
  28.1 33.4 %copy-start.7 = (bf16[2,2,128,256]{3,2,1,0:T(8,128)(2,1)}, bf16[2,2,128,256]{3,2,1,0:T(8,128)(2,1)S(1)}, u32[]{:S(2)}) copy-start(bf16[2,2,128,256]{3,2,1,0:T(8,128)(2,1)S(1)} %collective-permute-done.4.refs_1_) | copy-start | bytes 786436
  28.1 17.7 %collective-permute-start.5 = (bf16[2,2,128,256]{3,2,1,0:T(8,128)(2,1)S(1)}, bf16[2,2,128,256]{3,2,1,0:T(8,128)(2,1)S(1)}, u32[]{:S(2)}, u32[]{:S(2)}) collective-permute-start(bf16[2,2,128,256]{3,2,1,0:T(8,128)(2,1)S(1)} %collective-permute-done.4.refs_1_), channel_id=1, source_target_pairs={{0,4},{4,8},{8,12},{12,16},{16,20},{20,24},{24,28},{28,0},{1,5},{5... | collective-permute-start | bytes 786440 | tf_op jit(solution)/shard_map/ppermute | solution.py:499
  30.7 30.8 %copy-start.8 = (bf16[2,2,128,256]{3,2,1,0:T(8,128)(2,1)}, bf16[2,2,128,256]{3,2,1,0:T(8,128)(2,1)S(1)}, u32[]{:S(2)}) copy-start(bf16[2,2,128,256]{3,2,1,0:T(8,128)(2,1)S(1)} %collective-permute-done.9.refs_6_) | copy-start | bytes 786436
  30.7 15.4 %collective-permute-start.10 = (bf16[2,2,128,256]{3,2,1,0:T(8,128)(2,1)S(1)}, bf16[2,2,128,256]{3,2,1,0:T(8,128)(2,1)S(1)}, u32[]{:S(2)}, u32[]{:S(2)}) collective-permute-start(bf16[2,2,128,256]{3,2,1,0:T(8,128)(2,1)S(1)} %collective-permute-done.9.refs_6_), channel_id=1, source_target_pairs={{0,28},{4,0},{8,4},{12,8},{16,12},{20,16},{24,20},{28,24},{1,29},{... | collective-permute-start | bytes 786440 | tf_op jit(solution)/shard_map/ppermute | solution.py:499
  36.0 25.6 %all-to-all-start = ((bf16[8,136,512]{2,1,0:T(8,128)(2,1)}), bf16[8,136,512]{2,1,0:T(8,128)(2,1)S(1)}, u32[]{:S(2)}, u32[]{:S(2)}) async-start(bf16[8,136,512]{2,1,0:T(8,128)(2,1)} %queries_to_send.1), calls=%async_computation | async-start | bytes 2228224 | tf_op jit(solution)/shard_map/all_to_all | solution.py:508
  45.8 15.7 %copy-start.9 = (bf16[2,2,128,256]{3,2,1,0:T(8,128)(2,1)}, bf16[2,2,128,256]{3,2,1,0:T(8,128)(2,1)S(1)}, u32[]{:S(2)}) copy-start(bf16[2,2,128,256]{3,2,1,0:T(8,128)(2,1)S(1)} %collective-permute-done.5.refs_2_) | copy-start | bytes 786436
  45.9 9.1 %collective-permute-start.6 = (bf16[2,2,128,256]{3,2,1,0:T(8,128)(2,1)S(1)}, bf16[2,2,128,256]{3,2,1,0:T(8,128)(2,1)S(1)}, u32[]{:S(2)}, u32[]{:S(2)}) collective-permute-start(bf16[2,2,128,256]{3,2,1,0:T(8,128)(2,1)S(1)} %collective-permute-done.5.refs_2_), channel_id=1, source_target_pairs={{0,4},{4,8},{8,12},{12,16},{16,20},{20,24},{24,28},{28,0},{1,5},{5... | collective-permute-start | bytes 786440 | tf_op jit(solution)/shard_map/ppermute | solution.py:499
  46.1 15.4 %copy-start.3 = (bf16[2,2,128,256]{3,2,1,0:T(8,128)(2,1)}, bf16[2,2,128,256]{3,2,1,0:T(8,128)(2,1)S(1)}, u32[]{:S(2)}) copy-start(bf16[2,2,128,256]{3,2,1,0:T(8,128)(2,1)S(1)} %collective-permute-done.10.refs_5_) | copy-start | bytes 786436
  46.2 9.6 %collective-permute-start.11 = (bf16[2,128,256]{2,1,0:T(8,128)(2,1)S(1)}, bf16[2,128,256]{2,1,0:T(8,128)(2,1)S(1)}, u32[]{:S(2)}, u32[]{:S(2)}) collective-permute-start(bf16[2,128,256]{2,1,0:T(8,128)(2,1)S(1)} %slice_bitcast_fusion), channel_id=1, source_target_pairs={{0,28},{4,0},{8,4},{12,8},{16,12},{20,16},{24,20},{28,24},{1,29},{... | collective-permute-start | bytes 393224 | tf_op jit(solution)/shard_map/ppermute | solution.py:499
  55.0 6.6 %copy-start.4 = (bf16[2,2,128,256]{3,2,1,0:T(8,128)(2,1)}, bf16[2,2,128,256]{3,2,1,0:T(8,128)(2,1)S(1)}, u32[]{:S(2)}) copy-start(bf16[2,2,128,256]{3,2,1,0:T(8,128)(2,1)S(1)} %collective-permute-done.6.refs_3_) | copy-start | bytes 786436
  55.0 5.5 %collective-permute-start.7 = (bf16[2,128,256]{2,1,0:T(8,128)(2,1)S(1)}, bf16[2,128,256]{2,1,0:T(8,128)(2,1)S(1)}, u32[]{:S(2)}, u32[]{:S(2)}) collective-permute-start(bf16[2,128,256]{2,1,0:T(8,128)(2,1)S(1)} %slice_bitcast_fusion.1), channel_id=1, source_target_pairs={{0,4},{4,8},{8,12},{12,16},{16,20},{20,24},{24,28},{28,0},{1,5},{5... | collective-permute-start | bytes 393224 | tf_op jit(solution)/shard_map/ppermute | solution.py:499
  61.6 1.0 copy-start.1
  68.8 10.7 %all-to-all-start.2 = ((bf16[8,8,640]{2,1,0:T(8,128)(2,1)}), bf16[8,8,640]{2,1,0:T(8,128)(2,1)S(1)}, u32[]{:S(2)}, u32[]{:S(2)}) async-start(bf16[8,8,640]{2,1,0:T(8,128)(2,1)} %chosen_attention.1), calls=%async_computation.2 | async-start | bytes 163840 | tf_op jit(solution)/shard_map/all_to_all | solution.py:510
  74.6 14.0 %copy-start.10 = (bf16[4,2048]{1,0:T(4,128)(2,1)S(1)}, bf16[4,2048]{1,0:T(4,128)(2,1)}, u32[]{:S(2)}) copy-start(bf16[4,2048]{1,0:T(4,128)(2,1)} %param.17) | copy-start | bytes 49156
  74.6 17.1 %copy-start.12 = (f32[2048]{0:T(1024)S(1)}, f32[2048]{0:T(1024)}, u32[]{:S(2)}) copy-start(f32[2048]{0:T(1024)} %param.18) | copy-start | bytes 24580
  79.5 0.6 copy-start.5
  87.7 21.3 %copy-start.13 = (s32[512]{0:T(512)S(1)}, s32[512]{0:T(512)}, u32[]{:S(2)}) copy-start(s32[512]{0:T(512)} %param.21) | copy-start | bytes 6148
  88.7 2.9 %collective-permute-start.12 = (bf16[4,4096]{1,0:T(4,128)(2,1)S(1)}, bf16[4,4096]{1,0:T(4,128)(2,1)S(1)}, u32[]{:S(2)}, u32[]{:S(2)}) collective-permute-start(bf16[4,4096]{1,0:T(4,128)(2,1)S(1)} %convert_element_type.25), channel_id=1, source_target_pairs={{0,1},{1,0},{2,3},{3,2},{4,5},{5,4},{6,7},{7,6},{8,9},{9,8},{10,11... | collective-permute-start | bytes 98312 | tf_op jit(solution)/shard_map/ppermute | solution.py:43
  105.4 14.9 %all-to-all-start.4 = ((bf16[4,16,4,2048]{3,2,1,0:T(4,128)(2,1)}), bf16[4,16,4,2048]{3,2,1,0:T(4,128)(2,1)S(1)}, u32[]{:S(2)}, u32[]{:S(2)}) async-start(bf16[4,16,4,2048]{3,2,1,0:T(4,128)(2,1)} %broadcast_in_dim.14), calls=%async_computation.4 | async-start | bytes 2097152 | tf_op jit(solution)/shard_map/all_to_all | solution.py:37
  120.6 16.2 %collective-permute-start.14 = (bf16[256,2048]{1,0:T(8,128)(2,1)S(1)}, bf16[256,2048]{1,0:T(8,128)(2,1)}, u32[]{:S(2)}, u32[]{:S(2)}) collective-permute-start(bf16[256,2048]{1,0:T(8,128)(2,1)S(1)} %reshape.119), channel_id=1, source_target_pairs={{0,2},{2,0},{1,3},{3,1},{4,6},{6,4},{5,7},{7,5},{8,10},{10,8},{9,1... | collective-permute-start | bytes 3145736 | tf_op jit(solution)/shard_map/ppermute | solution.py:533
  128.8 7.8 %collective-permute-start.13 = (bf16[128,1002]{0,1:T(8,128)(2,1)S(1)}, bf16[128,1002]{0,1:T(8,128)(2,1)S(1)}, u32[]{:S(2)}, u32[]{:S(2)}) collective-permute-start(bf16[128,1002]{0,1:T(8,128)(2,1)S(1)} %dynamic-slice_convert_fusion.1), channel_id=1, source_target_pairs={{0,1},{1,0},{2,3},{3,2},{4,5},{5,4},{6,7},{7,6},{8,9},{9,8},{10,11... | collective-permute-start | bytes 769544 | tf_op jit(solution)/shard_map/ppermute | solution.py:43
  140.6 7.0 %collective-permute-start.15 = (bf16[128,1002]{0,1:T(8,128)(2,1)S(1)}, bf16[128,1002]{0,1:T(8,128)(2,1)S(1)}, u32[]{:S(2)}, u32[]{:S(2)}) collective-permute-start(bf16[128,1002]{0,1:T(8,128)(2,1)S(1)} %dynamic-slice_convert_fusion), channel_id=1, source_target_pairs={{0,1},{1,0},{2,3},{3,2},{4,5},{5,4},{6,7},{7,6},{8,9},{9,8},{10,11... | collective-permute-start | bytes 769544 | tf_op jit(solution)/shard_map/ppermute | solution.py:43
  148.6 17.6 %all-to-all-start.5 = ((f32[8,2,3,128]{3,1,2,0:T(2,128)}), f32[8,2,3,128]{3,1,2,0:T(2,128)S(1)}, u32[]{:S(2)}, u32[]{:S(2)}) async-start(f32[8,2,3,128]{3,1,2,0:T(2,128)} %broadcast_in_dim.16), calls=%async_computation.5 | async-start | bytes 49152 | tf_op jit(solution)/shard_map/all_to_all | solution.py:37
  166.2 36.5 %copy-start.14 = (f32[512]{0:T(512)S(1)}, f32[512]{0:T(512)}, u32[]{:S(2)}) copy-start(f32[512]{0:T(512)} %param.23) | copy-start | bytes 6148
  166.2 36.5 %copy-start.15 = (f32[512]{0:T(512)S(1)}, f32[512]{0:T(512)}, u32[]{:S(2)}) copy-start(f32[512]{0:T(512)} %param.22) | copy-start | bytes 6148
  166.3 23.5 %all-to-all-start.1 = ((bf16[8,128,640]{2,1,0:T(8,128)(2,1)}), bf16[8,128,640]{2,1,0:T(8,128)(2,1)S(1)}, u32[]{:S(2)}, u32[]{:S(2)}) async-start(bf16[8,128,640]{2,1,0:T(8,128)(2,1)} %partial_attention.5), calls=%async_computation.1 | async-start | bytes 2621440 | tf_op jit(solution)/shard_map/all_to_all | solution.py:515
  189.7 5.2 %copy-start = (bf16[8,128,640]{2,1,0:T(8,128)(2,1)}, bf16[8,128,640]{2,1,0:T(8,128)(2,1)S(1)}, u32[]{:S(2)}) copy-start(bf16[8,128,640]{2,1,0:T(8,128)(2,1)S(1)} %all-to-all-done.1.parts_ref) | copy-start | bytes 3932164
  190.4 11.9 %all-to-all-start.6 = ((f32[32,3,2,128]{3,2,1,0:T(2,128)}), f32[32,3,2,128]{3,2,1,0:T(2,128)S(1)}, u32[]{:S(2)}, u32[]{:S(2)}) async-start(f32[32,3,2,128]{3,2,1,0:T(2,128)} %broadcast_in_dim.17), calls=%async_computation.6 | async-start | bytes 196608 | tf_op jit(solution)/shard_map/all_to_all | solution.py:37
  202.8 0.6 copy-start.11

commit v3 on v2

--- a/solution.py
+++ b/solution.py
@@ -396,33 +396,51 @@
     merge_parts(parts_ref, merged_ref)
 
 
-def project_kernel(parts_ref, weight_ref, out_ref, chosen_ref):
-    @pl.when(pl.program_id(0) == 0)
+def project_kernel(parts_ref, *refs):
+    weight_refs = refs[:-3]
+    out_ref, merged_ref, chosen_ref = refs[-3:]
+    n = pl.program_id(0)
+    heads = chosen_ref.shape[0]
+
+    @pl.when(n == 0)
     def _():
-        merge_parts(parts_ref, chosen_ref)
-
-    out_ref[...] = jnp.dot(
-        chosen_ref[...], weight_ref[...], preferred_element_type=jnp.float32
-    )
-
-
-def projected_rows(parts, out_weight):
+        merge_parts(parts_ref, merged_ref)
+        for head in range(heads):
+            chosen_ref[head] = merged_ref[:, head * HEAD_SIZE : (head + 1) * HEAD_SIZE]
+        out_ref[...] = jnp.zeros(out_ref.shape, jnp.float32)
+
+    product = 0.0
+    for k, weight_ref in enumerate(weight_refs):
+        product = product + jnp.dot(
+            chosen_ref[n * len(weight_refs) + k],
+            weight_ref[...],
+            preferred_element_type=jnp.float32,
+        )
+    out_ref[...] += product[: out_ref.shape[0]]
+
+
+def projected_rows(parts, out_weight, count):
     rows = parts.shape[1]
     features, width = out_weight.shape
-    block = width // 8
+    heads = features // HEAD_SIZE
+    streams = 4
     return pl.pallas_call(
         project_kernel,
-        grid=(width // block,),
-        in_specs=[
-            pl.BlockSpec(parts.shape, lambda n: (0, 0, 0)),
-            pl.BlockSpec((features, block), lambda n: (0, n)),
+        grid=(heads // streams,),
+        in_specs=[pl.BlockSpec(parts.shape, lambda n: (0, 0, 0))]
+        + [
+            pl.BlockSpec((HEAD_SIZE, width), functools.partial(lambda k, n: (n * streams + k, 0), k))
+            for k in range(streams)
         ],
-        out_specs=pl.BlockSpec((rows, block), lambda n: (0, n)),
-        out_shape=jax.ShapeDtypeStruct((rows, width), jnp.float32),
-        scratch_shapes=[pltpu.VMEM((rows, features), jnp.bfloat16)],
+        out_specs=pl.BlockSpec((count, width), lambda n: (0, 0)),
+        out_shape=jax.ShapeDtypeStruct((count, width), jnp.float32),
+        scratch_shapes=[
+            pltpu.VMEM((rows, features), jnp.bfloat16),
+            pltpu.VMEM((heads, rows, HEAD_SIZE), jnp.bfloat16),
+        ],
         compiler_params=pltpu.CompilerParams(dimension_semantics=("arbitrary",)),
         name="projected_rows",
-    )(parts, out_weight)
+    )(parts, *[out_weight] * streams)
 
 
 def merged_attention(parts):
@@ -508,9 +526,9 @@
     q_all = lax.all_to_all(q_send, XC, 0, 0, tiled=True)
     few = chosen_attention(meta, q_all, kv_all)
     few = lax.all_to_all(few, XC, 0, 0, tiled=True)
-    partial_value = projected_rows(few, out_weight)[:count]
+    partial_value = projected_rows(few, out_weight, count)
     parts = q_all
-    for first, number in ((0, 1), (1, 1), (2, nx - 2)):
+    for first, number in ((0, 2), (2, nx - 2)):
         parts = partial_attention(meta, q_all, kv_all, first, number, parts)
     arrived = lax.all_to_all(parts, XC, 0, 0, tiled=True)
     attended = merged_attention(arrived)

time: 206 us -> 205 us (level)
  Pallas kernels: 43.7 us -> 37.4 us
  waiting for transfers between devices: 64.3 us -> 67.1 us
    all_to_all x3, waiting for transfers between devices: 10.4 us -> 15.3 us  [spread(): lax.all_to_all(jnp.broadcast_to(shard[None], (n, *shard.shape)), axes, 0,...]
    pallas_call x3 -> x2, Pallas kernels: 24.6 us -> 21.2 us  [partial_attention(): pl.pallas_call(functools.partial(attention_kernel, first), grid_spec=pltp...]
    pallas_call x1, Pallas kernels: 7.55 us -> 4.7 us  [projected_rows(): pl.pallas_call(project_kernel, grid=(heads // streams,), in_specs=[pl.Blo...]
    ppermute x3, waiting for transfers between devices: 10.6 us -> 8.42 us  [swap_heads(): return lax.ppermute(shard, 'head', [(0, 1), (1, 0)])]
  transfers between devices with their start and end apart: 22 -> 22, of which waited for: 14 -> 13; matrix products, arithmetic and copies ran while one was open for 3% -> 3% of each run, Pallas kernels for 15% -> 13%
where the time goes in v3:
time: 205 us; the launch traced here: 202 us
  waiting for transfers between devices  67.1 us (33%)
  starting transfers between devices  66.2 us (32%)
  Pallas kernels  37.4 us (18%)
  blocking collectives  12 us (6%)
  local copies, waits for them, and re-layouts  7.81 us (4%)
  matrix products  7.25 us (4%)
  other arithmetic  3.51 us (2%)
    pallas_call x2, Pallas kernels, partial_attention(): pl.pallas_call(functools.partial(attention_kernel, first), grid_spec=pltp...  21.2 us
    ppermute x8, starting transfers between devices, shifted(): return lax.ppermute(a, 'ctx_2', [(k, (k + d) % nz) for k in range(nz)])  18.7 us
    ppermute x8, waiting for transfers between devices, shifted(): return lax.ppermute(a, 'ctx_2', [(k, (k + d) % nz) for k in range(nz)])  18.2 us
    all_to_all x1, waiting for transfers between devices, per_device(): arrived = lax.all_to_all(parts, XC, 0, 0, tiled=True)  17.7 us
    all_to_all x3, waiting for transfers between devices, spread(): lax.all_to_all(jnp.broadcast_to(shard[None], (n, *shard.shape)), axes, 0,...  15.3 us
    all_to_all x3, starting transfers between devices, spread(): lax.all_to_all(jnp.broadcast_to(shard[None], (n, *shard.shape)), axes, 0,...  13.5 us
    all_to_all x1, blocking collectives, spread(): lax.all_to_all(jnp.broadcast_to(shard[None], (n, *shard.shape)), axes, 0,...  12 us
    all_to_all x1, starting transfers between devices, per_device(): q_all = lax.all_to_all(q_send, XC, 0, 0, tiled=True)  9.88 us
  transfers between devices with their start and end apart: 22, of which 13 were waited for; matrix products, arithmetic and copies ran while one was open for 3% of the time, Pallas kernels for 13%

profile of v3, /device:TPU:1, one launch (start us, length us, event | category | flops | bytes accessed | tf_op | source)
XLA Modules:
  0.0 202.3 jit_solution(6266752114480609433)
XLA Ops:
  0.6 0.8 constant_dynamic-slice_fusion.5
  1.5 4.4 %collective-permute-start.3 = (bf16[128,256]{1,0:T(8,128)(2,1)S(1)}, bf16[128,256]{1,0:T(8,128)(2,1)S(1)}, u32[]{:S(2)}, u32[]{:S(2)}) collective-permute-start(bf16[128,256]{1,0:T(8,128)(2,1)S(1)} %pad_maximum_fusion.3), channel_id=1, source_target_pairs={{0,34},{2,32},{4,102},{6,100},{8,170},{10,168},{12,238},{14,236},{... | collective-permute-start | bytes 196616 | tf_op jit(solution)/shard_map/ppermute | solution.py:513
  5.9 1.9 collective-permute-start.2
  7.7 0.7 collective-permute-start
  8.4 2.2 %collective-permute-done.2 = bf16[128,256]{1,0:T(8,128)(2,1)S(1)} collective-permute-done((bf16[128,256]{1,0:T(8,128)(2,1)S(1)}, bf16[128,256]{1,0:T(8,128)(2,1)S(1)}, u32[]{:S(2)}, u32[]{:S(2)}) %collective-permute-start.2) | collective-permute-done | bytes 65568 | tf_op jit(solution)/shard_map/ppermute | solution.py:513
  10.7 9.2 %collective-permute-start.8 = (bf16[2,2,128,256]{3,2,1,0:T(8,128)(2,1)S(1)}, bf16[2,2,128,256]{3,2,1,0:T(8,128)(2,1)S(1)}, u32[]{:S(2)}, u32[]{:S(2)}) collective-permute-start(bf16[2,2,128,256]{3,2,1,0:T(8,128)(2,1)S(1)} %bitcast.69), channel_id=1, source_target_pairs={{0,28},{4,0},{8,4},{12,8},{16,12},{20,16},{24,20},{28,24},{1,29},{... | collective-permute-start | bytes 786440 | tf_op jit(solution)/shard_map/ppermute | solution.py:517
  19.9 4.1 %collective-permute-done.8.refs_7_ = bf16[2,2,128,256]{3,2,1,0:T(8,128)(2,1)S(1)} collective-permute-done((bf16[2,2,128,256]{3,2,1,0:T(8,128)(2,1)S(1)}, bf16[2,2,128,256]{3,2,1,0:T(8,128)(2,1)S(1)}, u32[]{:S(2)}, u32[]{:S(2)}) %collective-permute-start.8) | collective-permute-done | bytes 262176 | tf_op jit(solution)/shard_map/ppermute | solution.py:517
  23.9 3.5 %collective-permute-start.9 = (bf16[2,2,128,256]{3,2,1,0:T(8,128)(2,1)S(1)}, bf16[2,2,128,256]{3,2,1,0:T(8,128)(2,1)S(1)}, u32[]{:S(2)}, u32[]{:S(2)}) collective-permute-start(bf16[2,2,128,256]{3,2,1,0:T(8,128)(2,1)S(1)} %collective-permute-done.8.refs_7_), channel_id=1, source_target_pairs={{0,28},{4,0},{8,4},{12,8},{16,12},{20,16},{24,20},{28,24},{1,29},{... | collective-permute-start | bytes 786440 | tf_op jit(solution)/shard_map/ppermute | solution.py:517
  27.4 0.7 collective-permute-done.4.refs_1_
  28.1 2.6 %collective-permute-done.9.refs_6_ = bf16[2,2,128,256]{3,2,1,0:T(8,128)(2,1)S(1)} collective-permute-done((bf16[2,2,128,256]{3,2,1,0:T(8,128)(2,1)S(1)}, bf16[2,2,128,256]{3,2,1,0:T(8,128)(2,1)S(1)}, u32[]{:S(2)}, u32[]{:S(2)}) %collective-permute-start.9) | collective-permute-done | bytes 262176 | tf_op jit(solution)/shard_map/ppermute | solution.py:517
  30.7 3.1 %collective-permute-start.10 = (bf16[2,2,128,256]{3,2,1,0:T(8,128)(2,1)S(1)}, bf16[2,2,128,256]{3,2,1,0:T(8,128)(2,1)S(1)}, u32[]{:S(2)}, u32[]{:S(2)}) collective-permute-start(bf16[2,2,128,256]{3,2,1,0:T(8,128)(2,1)S(1)} %collective-permute-done.9.refs_6_), channel_id=1, source_target_pairs={{0,28},{4,0},{8,4},{12,8},{16,12},{20,16},{24,20},{28,24},{1,29},{... | collective-permute-start | bytes 786440 | tf_op jit(solution)/shard_map/ppermute | solution.py:517
  33.8 2.1 %queries_to_send.1 = bf16[8,136,512]{2,1,0:T(8,128)(2,1)} custom-call(s32[4]{0:T(128)} %scored_ref.1, bf16[128,1024]{1,0:T(8,128)(2,1)} %q_ref.1), custom_call_target="tpu_custom_call" | custom-call | tf_op jit(solution)/shard_map/queries_to_send/pallas_call | solution.py:114
  36.0 9.9 %all-to-all-start = ((bf16[8,136,512]{2,1,0:T(8,128)(2,1)}), bf16[8,136,512]{2,1,0:T(8,128)(2,1)S(1)}, u32[]{:S(2)}, u32[]{:S(2)}) async-start(bf16[8,136,512]{2,1,0:T(8,128)(2,1)} %queries_to_send.1), calls=%async_computation | async-start | bytes 2228224 | tf_op jit(solution)/shard_map/all_to_all | solution.py:526
  46.2 2.7 %collective-permute-start.11 = (bf16[2,128,256]{2,1,0:T(8,128)(2,1)S(1)}, bf16[2,128,256]{2,1,0:T(8,128)(2,1)S(1)}, u32[]{:S(2)}, u32[]{:S(2)}) collective-permute-start(bf16[2,128,256]{2,1,0:T(8,128)(2,1)S(1)} %slice_bitcast_fusion), channel_id=1, source_target_pairs={{0,28},{4,0},{8,4},{12,8},{16,12},{20,16},{24,20},{28,24},{1,29},{... | collective-permute-start | bytes 393224 | tf_op jit(solution)/shard_map/ppermute | solution.py:517
  48.9 6.1 %collective-permute-done.6.refs_3_ = bf16[2,2,128,256]{3,2,1,0:T(8,128)(2,1)S(1)} collective-permute-done((bf16[2,2,128,256]{3,2,1,0:T(8,128)(2,1)S(1)}, bf16[2,2,128,256]{3,2,1,0:T(8,128)(2,1)S(1)}, u32[]{:S(2)}, u32[]{:S(2)}) %collective-permute-start.6) | collective-permute-done | bytes 262176 | tf_op jit(solution)/shard_map/ppermute | solution.py:517
  55.1 0.6 concatenate.17.meta_ref
  55.7 4.7 %collective-permute-done.7 = bf16[2,128,256]{2,1,0:T(8,128)(2,1)S(1)} collective-permute-done((bf16[2,128,256]{2,1,0:T(8,128)(2,1)S(1)}, bf16[2,128,256]{2,1,0:T(8,128)(2,1)S(1)}, u32[]{:S(2)}, u32[]{:S(2)}) %collective-permute-start.7) | collective-permute-done | bytes 131104 | tf_op jit(solution)/shard_map/ppermute | solution.py:517
  60.5 0.7 pad_maximum_fusion.1.refs_4_
  61.6 1.0 copy-done.1
  62.6 6.2 %chosen_attention.1 = bf16[8,8,640]{2,1,0:T(8,128)(2,1)} custom-call(s32[12]{0:T(128)} %concatenate.17.meta_ref, bf16[8,136,512]{2,1,0:T(8,128)(2,1)} %copy-done.1, bf16[2,2,128,256]{3,2,1,0:T(8,128)(2,1)} %bitcast.71, bf16[2,2,128,256]{3,2,1,0:T(8,128)(2,1)} %copy-done.7, bf16[2,2,128,256]{3,2,1,0:T(8,128)(2,1)} %copy-done.9, ...), custom_call_target="tpu_custom_call" | custom-call | tf_op jit(solution)/shard_map/chosen_attention/pallas_call | solution.py:212
  68.8 5.8 %all-to-all-start.2 = ((bf16[8,8,640]{2,1,0:T(8,128)(2,1)}), bf16[8,8,640]{2,1,0:T(8,128)(2,1)S(1)}, u32[]{:S(2)}, u32[]{:S(2)}) async-start(bf16[8,8,640]{2,1,0:T(8,128)(2,1)} %chosen_attention.1), calls=%async_computation.2 | async-start | bytes 163840 | tf_op jit(solution)/shard_map/all_to_all | solution.py:528
  74.6 4.9 %all-to-all-done.2.parts_ref = bf16[8,8,640]{2,1,0:T(8,128)(2,1)S(1)} async-done(((bf16[8,8,640]{2,1,0:T(8,128)(2,1)}), bf16[8,8,640]{2,1,0:T(8,128)(2,1)S(1)}, u32[]{:S(2)}, u32[]{:S(2)}) %all-to-all-start.2) | async-done | bytes 81952 | tf_op jit(solution)/shard_map/all_to_all | solution.py:528
  79.5 0.6 copy-done.5
  80.1 4.7 %projected_rows.1 = f32[4,4096]{1,0:T(4,128)} custom-call(bf16[8,8,640]{2,1,0:T(8,128)(2,1)} %copy-done.5, bf16[1024,4096]{1,0:T(8,128)(2,1)} %refs_3_.1, bf16[1024,4096]{1,0:T(8,128)(2,1)} %refs_3_.1, bf16[1024,4096]{1,0:T(8,128)(2,1)} %refs_3_.1, bf16[1024,4096]{1,0:T(8,128)(2,1)} %refs_3_.1), custom_call_target="tpu_custom_call" | custom-call | tf_op jit(solution)/shard_map/projected_rows/pallas_call | solution.py:427
  84.8 0.9 copy.62
  85.8 2.8 %collective-permute-done.12 = bf16[4,4096]{1,0:T(4,128)(2,1)S(1)} collective-permute-done((bf16[4,4096]{1,0:T(4,128)(2,1)S(1)}, bf16[4,4096]{1,0:T(4,128)(2,1)S(1)}, u32[]{:S(2)}, u32[]{:S(2)}) %collective-permute-start.12) | collective-permute-done | bytes 32800 | tf_op jit(solution)/shard_map/ppermute | solution.py:43
  88.8 0.8 multiply_convert_fusion
  89.7 12.0 %all_to_all.35 = bf16[16,4,2048]{2,1,0:T(4,128)(2,1)S(1)} all-to-all(bf16[16,4,2048]{2,1,0:T(4,128)(2,1)S(1)} %broadcast_in_dim.12), channel_id=1, replica_groups=mesh['ctx_0'=4,'ctx_1'=2,'ctx_2'=8,'ctx_3'=2,'head'=2] {'ctx_1','ctx_2'}, dimensions={0} | all-to-all | bytes 524288 | tf_op jit(solution)/shard_map/all_to_all | solution.py:37
  101.7 1.5 broadcast_in_dim.14
  103.2 3.5 %all-to-all-start.4 = ((bf16[4,16,4,2048]{3,2,1,0:T(4,128)(2,1)}), bf16[4,16,4,2048]{3,2,1,0:T(4,128)(2,1)S(1)}, u32[]{:S(2)}, u32[]{:S(2)}) async-start(bf16[4,16,4,2048]{3,2,1,0:T(4,128)(2,1)} %broadcast_in_dim.14), calls=%async_computation.4 | async-start | bytes 2097152 | tf_op jit(solution)/shard_map/all_to_all | solution.py:37
  107.0 11.1 %all-to-all-done.4 = bf16[4,16,4,2048]{3,2,1,0:T(4,128)(2,1)S(1)} async-done(((bf16[4,16,4,2048]{3,2,1,0:T(4,128)(2,1)}), bf16[4,16,4,2048]{3,2,1,0:T(4,128)(2,1)S(1)}, u32[]{:S(2)}, u32[]{:S(2)}) %all-to-all-start.4) | async-done | bytes 1048608 | tf_op jit(solution)/shard_map/all_to_all | solution.py:37
  118.3 4.7 %collective-permute-start.14 = (bf16[256,2048]{1,0:T(8,128)(2,1)S(1)}, bf16[256,2048]{1,0:T(8,128)(2,1)}, u32[]{:S(2)}, u32[]{:S(2)}) collective-permute-start(bf16[256,2048]{1,0:T(8,128)(2,1)S(1)} %reshape.119), channel_id=1, source_target_pairs={{0,2},{2,0},{1,3},{3,1},{4,6},{6,4},{5,7},{7,5},{8,10},{10,8},{9,1... | collective-permute-start | bytes 3145736 | tf_op jit(solution)/shard_map/ppermute | solution.py:551
  123.0 3.5 %fusion.13 = f32[256,1002]{0,1:T(8,128)S(1)} fusion(bf16[256,2048]{1,0:T(8,128)(2,1)S(1)} %reshape.119, bf16[2048,1002]{0,1:T(8,128)(2,1)} %param.20), kind=kOutput, calls=%fused_computation.56 | convolution fusion | flops 1050673152 | bytes 6178816 | tf_op jit(solution)/shard_map/dot_general | solution.py:560
  126.6 0.5 collective-permute-start.13
  127.1 7.4 %partial_attention.2.refs_8_ = bf16[8,128,640]{2,1,0:T(8,128)(2,1)} custom-call(s32[12]{0:T(128)} %concatenate.17.meta_ref, bf16[8,136,512]{2,1,0:T(8,128)(2,1)} %copy-done.1, bf16[2,2,128,256]{3,2,1,0:T(8,128)(2,1)} %bitcast.72, bf16[2,2,128,256]{3,2,1,0:T(8,128)(2,1)} %copy-done.7, bf16[2,2,128,256]{3,2,1,0:T(8,128)(2,1)} %copy-done.9, ...), custom_call_target="tpu_custom_call" | custom-call | flops 10000000000 | bytes 4000000 | tf_op jit(solution)/shard_map/partial_attention/pallas_call | solution.py:339
  134.6 3.8 %fusion.14 = f32[256,1002]{0,1:T(8,128)S(1)} fusion(bf16[256,2048]{1,0:T(8,128)(2,1)} %collective-permute-done.14, bf16[2048,1002]{0,1:T(8,128)(2,1)} %param.20), kind=kOutput, calls=%fused_computation.57 | convolution fusion | flops 1050673152 | bytes 6178816 | tf_op jit(solution)/shard_map/dot_general | solution.py:560
  138.5 1.2 collective-permute-start.15
  139.8 5.7 %collective-permute-done.15 = bf16[128,1002]{0,1:T(8,128)(2,1)S(1)} collective-permute-done((bf16[128,1002]{0,1:T(8,128)(2,1)S(1)}, bf16[128,1002]{0,1:T(8,128)(2,1)S(1)}, u32[]{:S(2)}, u32[]{:S(2)}) %collective-permute-start.15) | collective-permute-done | bytes 256544 | tf_op jit(solution)/shard_map/ppermute | solution.py:43
  145.9 0.6 broadcast_in_dim.16
  146.5 5.5 %all-to-all-start.5 = ((f32[8,2,3,128]{3,1,2,0:T(2,128)}), f32[8,2,3,128]{3,1,2,0:T(2,128)S(1)}, u32[]{:S(2)}, u32[]{:S(2)}) async-start(f32[8,2,3,128]{3,1,2,0:T(2,128)} %broadcast_in_dim.16), calls=%async_computation.5 | async-start | bytes 49152 | tf_op jit(solution)/shard_map/all_to_all | solution.py:37
  152.0 13.8 %partial_attention.3 = bf16[8,128,640]{2,1,0:T(8,128)(2,1)} custom-call(s32[12]{0:T(128)} %concatenate.17.meta_ref, bf16[8,136,512]{2,1,0:T(8,128)(2,1)} %copy-done.1, bf16[2,2,128,256]{3,2,1,0:T(8,128)(2,1)} %bitcast.73, bf16[2,2,128,256]{3,2,1,0:T(8,128)(2,1)} %copy-done.7, bf16[2,2,128,256]{3,2,1,0:T(8,128)(2,1)} %copy-done.9, ...), custom_call_target="tpu_custom_call", output_to_operand_aliasing={{}: (10, {})} | custom-call | flops 10000000000 | bytes 4000000 | tf_op jit(solution)/shard_map/partial_attention/pallas_call | solution.py:339
  165.8 5.0 %all-to-all-start.1 = ((bf16[8,128,640]{2,1,0:T(8,128)(2,1)}), bf16[8,128,640]{2,1,0:T(8,128)(2,1)S(1)}, u32[]{:S(2)}, u32[]{:S(2)}) async-start(bf16[8,128,640]{2,1,0:T(8,128)(2,1)} %partial_attention.3), calls=%async_computation.1 | async-start | bytes 2621440 | tf_op jit(solution)/shard_map/all_to_all | solution.py:533
  170.9 17.7 %all-to-all-done.1.parts_ref = bf16[8,128,640]{2,1,0:T(8,128)(2,1)S(1)} async-done(((bf16[8,128,640]{2,1,0:T(8,128)(2,1)}), bf16[8,128,640]{2,1,0:T(8,128)(2,1)S(1)}, u32[]{:S(2)}, u32[]{:S(2)}) %all-to-all-start.1) | async-done | bytes 1310752 | tf_op jit(solution)/shard_map/all_to_all | solution.py:533
  188.6 0.7 broadcast_in_dim.17
  189.3 4.5 %all-to-all-start.6 = ((f32[32,3,2,128]{3,2,1,0:T(2,128)}), f32[32,3,2,128]{3,2,1,0:T(2,128)S(1)}, u32[]{:S(2)}, u32[]{:S(2)}) async-start(f32[32,3,2,128]{3,2,1,0:T(2,128)} %broadcast_in_dim.17), calls=%async_computation.6 | async-start | bytes 196608 | tf_op jit(solution)/shard_map/all_to_all | solution.py:37
  193.8 3.2 %merged_attention.1 = bf16[128,1024]{1,0:T(8,128)(2,1)} custom-call(bf16[8,128,640]{2,1,0:T(8,128)(2,1)} %copy-done), custom_call_target="tpu_custom_call" | custom-call | tf_op jit(solution)/shard_map/merged_attention/pallas_call | solution.py:448
  197.0 4.2 %all-to-all-done.6 = f32[32,3,2,128]{3,2,1,0:T(2,128)S(1)} async-done(((f32[32,3,2,128]{3,2,1,0:T(2,128)}), f32[32,3,2,128]{3,2,1,0:T(2,128)S(1)}, u32[]{:S(2)}, u32[]{:S(2)}) %all-to-all-start.6) | async-done | bytes 98336 | tf_op jit(solution)/shard_map/all_to_all | solution.py:37
  201.7 0.6 minimum_negate_fusion
  (88 shorter events, 3.0 us)
Async XLA Ops:
  0.6 45.3 %copy-start.16 = (s32[8]{0:T(128)S(1)}, s32[8]{0:T(128)}, u32[]{:S(2)}) copy-start(s32[8]{0:T(128)} %param.15) | copy-start | bytes 100
  1.5 6.9 %collective-permute-start.3 = (bf16[128,256]{1,0:T(8,128)(2,1)S(1)}, bf16[128,256]{1,0:T(8,128)(2,1)S(1)}, u32[]{:S(2)}, u32[]{:S(2)}) collective-permute-start(bf16[128,256]{1,0:T(8,128)(2,1)S(1)} %pad_maximum_fusion.3), channel_id=1, source_target_pairs={{0,34},{2,32},{4,102},{6,100},{8,170},{10,168},{12,238},{14,236},{... | collective-permute-start | bytes 196616 | tf_op jit(solution)/shard_map/ppermute | solution.py:513
  5.9 2.5 %collective-permute-start.1 = (bf16[128,256]{1,0:T(8,128)(2,1)S(1)}, bf16[128,256]{1,0:T(8,128)(2,1)S(1)}, u32[]{:S(2)}, u32[]{:S(2)}) collective-permute-start(bf16[128,256]{1,0:T(8,128)(2,1)S(1)} %pad_maximum_fusion.3), channel_id=1, source_target_pairs={{0,2},{2,0},{4,70},{6,68},{8,138},{10,136},{12,206},{14,204},{16,1... | collective-permute-start | bytes 196616 | tf_op jit(solution)/shard_map/ppermute | solution.py:513
  5.9 4.7 %collective-permute-start.2 = (bf16[128,256]{1,0:T(8,128)(2,1)S(1)}, bf16[128,256]{1,0:T(8,128)(2,1)S(1)}, u32[]{:S(2)}, u32[]{:S(2)}) collective-permute-start(bf16[128,256]{1,0:T(8,128)(2,1)S(1)} %pad_maximum_fusion.2), channel_id=1, source_target_pairs={{0,32},{2,34},{4,100},{6,102},{8,168},{10,170},{12,236},{14,238},{... | collective-permute-start | bytes 196616 | tf_op jit(solution)/shard_map/ppermute | solution.py:513
  7.7 2.9 %collective-permute-start = (bf16[128,256]{1,0:T(8,128)(2,1)S(1)}, bf16[128,256]{1,0:T(8,128)(2,1)S(1)}, u32[]{:S(2)}, u32[]{:S(2)}) collective-permute-start(bf16[128,256]{1,0:T(8,128)(2,1)S(1)} %pad_maximum_fusion.2), channel_id=1, source_target_pairs={{0,0},{2,2},{4,68},{6,70},{8,136},{10,138},{12,204},{14,206},{16,1... | collective-permute-start | bytes 196616 | tf_op jit(solution)/shard_map/ppermute | solution.py:513
  10.6 50.9 %copy-start.2 = (bf16[4,128,256]{2,1,0:T(8,128)(2,1)}, bf16[4,128,256]{2,1,0:T(8,128)(2,1)S(1)}, u32[]{:S(2)}) copy-start(bf16[4,128,256]{2,1,0:T(8,128)(2,1)S(1)} %pad_maximum_fusion) | copy-start | bytes 786436
  10.7 13.3 %collective-permute-start.8 = (bf16[2,2,128,256]{3,2,1,0:T(8,128)(2,1)S(1)}, bf16[2,2,128,256]{3,2,1,0:T(8,128)(2,1)S(1)}, u32[]{:S(2)}, u32[]{:S(2)}) collective-permute-start(bf16[2,2,128,256]{3,2,1,0:T(8,128)(2,1)S(1)} %bitcast.69), channel_id=1, source_target_pairs={{0,28},{4,0},{8,4},{12,8},{16,12},{20,16},{24,20},{28,24},{1,29},{... | collective-permute-start | bytes 786440 | tf_op jit(solution)/shard_map/ppermute | solution.py:517
  19.9 8.3 %collective-permute-start.4 = (bf16[2,2,128,256]{3,2,1,0:T(8,128)(2,1)S(1)}, bf16[2,2,128,256]{3,2,1,0:T(8,128)(2,1)S(1)}, u32[]{:S(2)}, u32[]{:S(2)}) collective-permute-start(bf16[2,2,128,256]{3,2,1,0:T(8,128)(2,1)S(1)} %bitcast.70), channel_id=1, source_target_pairs={{0,4},{4,8},{8,12},{12,16},{16,20},{20,24},{24,28},{28,0},{1,5},{5... | collective-permute-start | bytes 786440 | tf_op jit(solution)/shard_map/ppermute | solution.py:517
  23.9 37.6 %copy-start.6 = (bf16[2,2,128,256]{3,2,1,0:T(8,128)(2,1)}, bf16[2,2,128,256]{3,2,1,0:T(8,128)(2,1)S(1)}, u32[]{:S(2)}) copy-start(bf16[2,2,128,256]{3,2,1,0:T(8,128)(2,1)S(1)} %collective-permute-done.8.refs_7_) | copy-start | bytes 786436
  23.9 6.8 %collective-permute-start.9 = (bf16[2,2,128,256]{3,2,1,0:T(8,128)(2,1)S(1)}, bf16[2,2,128,256]{3,2,1,0:T(8,128)(2,1)S(1)}, u32[]{:S(2)}, u32[]{:S(2)}) collective-permute-start(bf16[2,2,128,256]{3,2,1,0:T(8,128)(2,1)S(1)} %collective-permute-done.8.refs_7_), channel_id=1, source_target_pairs={{0,28},{4,0},{8,4},{12,8},{16,12},{20,16},{24,20},{28,24},{1,29},{... | collective-permute-start | bytes 786440 | tf_op jit(solution)/shard_map/ppermute | solution.py:517
  28.1 33.4 %copy-start.7 = (bf16[2,2,128,256]{3,2,1,0:T(8,128)(2,1)}, bf16[2,2,128,256]{3,2,1,0:T(8,128)(2,1)S(1)}, u32[]{:S(2)}) copy-start(bf16[2,2,128,256]{3,2,1,0:T(8,128)(2,1)S(1)} %collective-permute-done.4.refs_1_) | copy-start | bytes 786436
  28.1 17.7 %collective-permute-start.5 = (bf16[2,2,128,256]{3,2,1,0:T(8,128)(2,1)S(1)}, bf16[2,2,128,256]{3,2,1,0:T(8,128)(2,1)S(1)}, u32[]{:S(2)}, u32[]{:S(2)}) collective-permute-start(bf16[2,2,128,256]{3,2,1,0:T(8,128)(2,1)S(1)} %collective-permute-done.4.refs_1_), channel_id=1, source_target_pairs={{0,4},{4,8},{8,12},{12,16},{16,20},{20,24},{24,28},{28,0},{1,5},{5... | collective-permute-start | bytes 786440 | tf_op jit(solution)/shard_map/ppermute | solution.py:517
  30.7 30.8 %copy-start.8 = (bf16[2,2,128,256]{3,2,1,0:T(8,128)(2,1)}, bf16[2,2,128,256]{3,2,1,0:T(8,128)(2,1)S(1)}, u32[]{:S(2)}) copy-start(bf16[2,2,128,256]{3,2,1,0:T(8,128)(2,1)S(1)} %collective-permute-done.9.refs_6_) | copy-start | bytes 786436
  30.7 15.4 %collective-permute-start.10 = (bf16[2,2,128,256]{3,2,1,0:T(8,128)(2,1)S(1)}, bf16[2,2,128,256]{3,2,1,0:T(8,128)(2,1)S(1)}, u32[]{:S(2)}, u32[]{:S(2)}) collective-permute-start(bf16[2,2,128,256]{3,2,1,0:T(8,128)(2,1)S(1)} %collective-permute-done.9.refs_6_), channel_id=1, source_target_pairs={{0,28},{4,0},{8,4},{12,8},{16,12},{20,16},{24,20},{28,24},{1,29},{... | collective-permute-start | bytes 786440 | tf_op jit(solution)/shard_map/ppermute | solution.py:517
  36.0 25.6 %all-to-all-start = ((bf16[8,136,512]{2,1,0:T(8,128)(2,1)}), bf16[8,136,512]{2,1,0:T(8,128)(2,1)S(1)}, u32[]{:S(2)}, u32[]{:S(2)}) async-start(bf16[8,136,512]{2,1,0:T(8,128)(2,1)} %queries_to_send.1), calls=%async_computation | async-start | bytes 2228224 | tf_op jit(solution)/shard_map/all_to_all | solution.py:526
  45.8 15.7 %copy-start.9 = (bf16[2,2,128,256]{3,2,1,0:T(8,128)(2,1)}, bf16[2,2,128,256]{3,2,1,0:T(8,128)(2,1)S(1)}, u32[]{:S(2)}) copy-start(bf16[2,2,128,256]{3,2,1,0:T(8,128)(2,1)S(1)} %collective-permute-done.5.refs_2_) | copy-start | bytes 786436
  45.9 9.1 %collective-permute-start.6 = (bf16[2,2,128,256]{3,2,1,0:T(8,128)(2,1)S(1)}, bf16[2,2,128,256]{3,2,1,0:T(8,128)(2,1)S(1)}, u32[]{:S(2)}, u32[]{:S(2)}) collective-permute-start(bf16[2,2,128,256]{3,2,1,0:T(8,128)(2,1)S(1)} %collective-permute-done.5.refs_2_), channel_id=1, source_target_pairs={{0,4},{4,8},{8,12},{12,16},{16,20},{20,24},{24,28},{28,0},{1,5},{5... | collective-permute-start | bytes 786440 | tf_op jit(solution)/shard_map/ppermute | solution.py:517
  46.1 15.4 %copy-start.3 = (bf16[2,2,128,256]{3,2,1,0:T(8,128)(2,1)}, bf16[2,2,128,256]{3,2,1,0:T(8,128)(2,1)S(1)}, u32[]{:S(2)}) copy-start(bf16[2,2,128,256]{3,2,1,0:T(8,128)(2,1)S(1)} %collective-permute-done.10.refs_5_) | copy-start | bytes 786436
  46.2 9.6 %collective-permute-start.11 = (bf16[2,128,256]{2,1,0:T(8,128)(2,1)S(1)}, bf16[2,128,256]{2,1,0:T(8,128)(2,1)S(1)}, u32[]{:S(2)}, u32[]{:S(2)}) collective-permute-start(bf16[2,128,256]{2,1,0:T(8,128)(2,1)S(1)} %slice_bitcast_fusion), channel_id=1, source_target_pairs={{0,28},{4,0},{8,4},{12,8},{16,12},{20,16},{24,20},{28,24},{1,29},{... | collective-permute-start | bytes 393224 | tf_op jit(solution)/shard_map/ppermute | solution.py:517
  55.0 6.6 %copy-start.4 = (bf16[2,2,128,256]{3,2,1,0:T(8,128)(2,1)}, bf16[2,2,128,256]{3,2,1,0:T(8,128)(2,1)S(1)}, u32[]{:S(2)}) copy-start(bf16[2,2,128,256]{3,2,1,0:T(8,128)(2,1)S(1)} %collective-permute-done.6.refs_3_) | copy-start | bytes 786436
  55.0 5.5 %collective-permute-start.7 = (bf16[2,128,256]{2,1,0:T(8,128)(2,1)S(1)}, bf16[2,128,256]{2,1,0:T(8,128)(2,1)S(1)}, u32[]{:S(2)}, u32[]{:S(2)}) collective-permute-start(bf16[2,128,256]{2,1,0:T(8,128)(2,1)S(1)} %slice_bitcast_fusion.1), channel_id=1, source_target_pairs={{0,4},{4,8},{8,12},{12,16},{16,20},{20,24},{24,28},{28,0},{1,5},{5... | collective-permute-start | bytes 393224 | tf_op jit(solution)/shard_map/ppermute | solution.py:517
  61.6 1.0 copy-start.1
  68.8 10.7 %all-to-all-start.2 = ((bf16[8,8,640]{2,1,0:T(8,128)(2,1)}), bf16[8,8,640]{2,1,0:T(8,128)(2,1)S(1)}, u32[]{:S(2)}, u32[]{:S(2)}) async-start(bf16[8,8,640]{2,1,0:T(8,128)(2,1)} %chosen_attention.1), calls=%async_computation.2 | async-start | bytes 163840 | tf_op jit(solution)/shard_map/all_to_all | solution.py:528
  74.6 11.1 %copy-start.10 = (bf16[4,2048]{1,0:T(4,128)(2,1)S(1)}, bf16[4,2048]{1,0:T(4,128)(2,1)}, u32[]{:S(2)}) copy-start(bf16[4,2048]{1,0:T(4,128)(2,1)} %param.17) | copy-start | bytes 49156
  74.6 14.2 %copy-start.12 = (f32[2048]{0:T(1024)S(1)}, f32[2048]{0:T(1024)}, u32[]{:S(2)}) copy-start(f32[2048]{0:T(1024)} %param.18) | copy-start | bytes 24580
  79.5 0.6 copy-start.5
  84.8 21.9 %copy-start.13 = (s32[512]{0:T(512)S(1)}, s32[512]{0:T(512)}, u32[]{:S(2)}) copy-start(s32[512]{0:T(512)} %param.21) | copy-start | bytes 6148
  85.7 2.9 %collective-permute-start.12 = (bf16[4,4096]{1,0:T(4,128)(2,1)S(1)}, bf16[4,4096]{1,0:T(4,128)(2,1)S(1)}, u32[]{:S(2)}, u32[]{:S(2)}) collective-permute-start(bf16[4,4096]{1,0:T(4,128)(2,1)S(1)} %convert_element_type.25), channel_id=1, source_target_pairs={{0,1},{1,0},{2,3},{3,2},{4,5},{5,4},{6,7},{7,6},{8,9},{9,8},{10,11... | collective-permute-start | bytes 98312 | tf_op jit(solution)/shard_map/ppermute | solution.py:43
  103.2 14.9 %all-to-all-start.4 = ((bf16[4,16,4,2048]{3,2,1,0:T(4,128)(2,1)}), bf16[4,16,4,2048]{3,2,1,0:T(4,128)(2,1)S(1)}, u32[]{:S(2)}, u32[]{:S(2)}) async-start(bf16[4,16,4,2048]{3,2,1,0:T(4,128)(2,1)} %broadcast_in_dim.14), calls=%async_computation.4 | async-start | bytes 2097152 | tf_op jit(solution)/shard_map/all_to_all | solution.py:37
  118.3 16.3 %collective-permute-start.14 = (bf16[256,2048]{1,0:T(8,128)(2,1)S(1)}, bf16[256,2048]{1,0:T(8,128)(2,1)}, u32[]{:S(2)}, u32[]{:S(2)}) collective-permute-start(bf16[256,2048]{1,0:T(8,128)(2,1)S(1)} %reshape.119), channel_id=1, source_target_pairs={{0,2},{2,0},{1,3},{3,1},{4,6},{6,4},{5,7},{7,5},{8,10},{10,8},{9,1... | collective-permute-start | bytes 3145736 | tf_op jit(solution)/shard_map/ppermute | solution.py:551
  126.6 7.9 %collective-permute-start.13 = (bf16[128,1002]{0,1:T(8,128)(2,1)S(1)}, bf16[128,1002]{0,1:T(8,128)(2,1)S(1)}, u32[]{:S(2)}, u32[]{:S(2)}) collective-permute-start(bf16[128,1002]{0,1:T(8,128)(2,1)S(1)} %dynamic-slice_convert_fusion.1), channel_id=1, source_target_pairs={{0,1},{1,0},{2,3},{3,2},{4,5},{5,4},{6,7},{7,6},{8,9},{9,8},{10,11... | collective-permute-start | bytes 769544 | tf_op jit(solution)/shard_map/ppermute | solution.py:43
  138.5 7.0 %collective-permute-start.15 = (bf16[128,1002]{0,1:T(8,128)(2,1)S(1)}, bf16[128,1002]{0,1:T(8,128)(2,1)S(1)}, u32[]{:S(2)}, u32[]{:S(2)}) collective-permute-start(bf16[128,1002]{0,1:T(8,128)(2,1)S(1)} %dynamic-slice_convert_fusion), channel_id=1, source_target_pairs={{0,1},{1,0},{2,3},{3,2},{4,5},{5,4},{6,7},{7,6},{8,9},{9,8},{10,11... | collective-permute-start | bytes 769544 | tf_op jit(solution)/shard_map/ppermute | solution.py:43
  146.5 19.3 %all-to-all-start.5 = ((f32[8,2,3,128]{3,1,2,0:T(2,128)}), f32[8,2,3,128]{3,1,2,0:T(2,128)S(1)}, u32[]{:S(2)}, u32[]{:S(2)}) async-start(f32[8,2,3,128]{3,1,2,0:T(2,128)} %broadcast_in_dim.16), calls=%async_computation.5 | async-start | bytes 49152 | tf_op jit(solution)/shard_map/all_to_all | solution.py:37
  165.7 35.9 %copy-start.14 = (f32[512]{0:T(512)S(1)}, f32[512]{0:T(512)}, u32[]{:S(2)}) copy-start(f32[512]{0:T(512)} %param.23) | copy-start | bytes 6148
  165.8 35.9 %copy-start.15 = (f32[512]{0:T(512)S(1)}, f32[512]{0:T(512)}, u32[]{:S(2)}) copy-start(f32[512]{0:T(512)} %param.22) | copy-start | bytes 6148
  165.8 22.8 %all-to-all-start.1 = ((bf16[8,128,640]{2,1,0:T(8,128)(2,1)}), bf16[8,128,640]{2,1,0:T(8,128)(2,1)S(1)}, u32[]{:S(2)}, u32[]{:S(2)}) async-start(bf16[8,128,640]{2,1,0:T(8,128)(2,1)} %partial_attention.3), calls=%async_computation.1 | async-start | bytes 2621440 | tf_op jit(solution)/shard_map/all_to_all | solution.py:533
  188.6 5.2 %copy-start = (bf16[8,128,640]{2,1,0:T(8,128)(2,1)}, bf16[8,128,640]{2,1,0:T(8,128)(2,1)S(1)}, u32[]{:S(2)}) copy-start(bf16[8,128,640]{2,1,0:T(8,128)(2,1)S(1)} %all-to-all-done.1.parts_ref) | copy-start | bytes 3932164
  189.3 11.9 %all-to-all-start.6 = ((f32[32,3,2,128]{3,2,1,0:T(2,128)}), f32[32,3,2,128]{3,2,1,0:T(2,128)S(1)}, u32[]{:S(2)}, u32[]{:S(2)}) async-start(f32[32,3,2,128]{3,2,1,0:T(2,128)} %broadcast_in_dim.17), calls=%async_computation.6 | async-start | bytes 196608 | tf_op jit(solution)/shard_map/all_to_all | solution.py:37
  201.7 0.6 copy-start.11
